TPU v7x, 32 devices: a whole 2x2x4 slice. The times are simulated.
32 devices in a mesh: dp: 16 (over z, x, core), head: 2 (over y).
Axes of the slice: x: 2, y: 2, z: 4, core: 2. Of those that a mesh axis runs over, the one named last changes fastest.
Arguments:
- layer_in: bfloat16 [4096, 1536], P('dp'), may hold values from -6 to 6
- gain_attn: bfloat16 [1536], replicated, may hold values from 0.5 to 1.5
- q_weight: bfloat16 [1536, 1536], P('dp', 'head'), may hold values from -0.15625 to 0.15625
- q_bias: bfloat16 [1536], P('head'), may hold values from -3 to 3
- key_weight: bfloat16 [1536, 256], P('dp', 'head'), may hold values from -0.15625 to 0.15625
- key_bias: bfloat16 [256], P('head'), may hold values from -3 to 3
- value_weight: bfloat16 [1536, 256], P('dp', 'head'), may hold values from -0.15625 to 0.15625
- value_bias: bfloat16 [256], P('head'), may hold values from -3 to 3
- o_weight: bfloat16 [1536, 1536], P('head', 'dp'), may hold values from -0.875 to 0.875
- gain_mlp: bfloat16 [1536], replicated, may hold values from 0.5 to 1.5
- gate_weight: bfloat16 [1536, 8960], P('dp', 'head'), may hold values from -0.15625 to 0.15625
- up_weight: bfloat16 [1536, 8960], P('dp', 'head'), may hold values from -0.15625 to 0.15625
- down_weight: bfloat16 [8960, 1536], P('head', 'dp'), may hold values from -0.0625 to 0.0625
- row_lengths: int32 [3], replicated, may hold values from 1 to 2048, 4096 in all
- source_ids: int32 [4096], P('dp'), may hold values from 0 to 7
- source_weights: int32 [8], replicated, may hold values from 4 to 32
- out_grad: bfloat16 [4096, 1536], P('dp'), may hold values from -6 to 6
Outputs:
- layer_out: bfloat16 [4096, 1536], P('dp')
- layer_in_grad: bfloat16 [4096, 1536], P('dp')
- gain_attn_grad: float32 [1536], replicated
- q_weight_grad: float32 [1536, 1536], P('dp', 'head')
- q_bias_grad: float32 [1536], P('head')
- k_weight_grad: float32 [1536, 256], P('dp', 'head')
- k_bias_grad: float32 [256], P('head')
- v_weight_grad: float32 [1536, 256], P('dp', 'head')
- v_bias_grad: float32 [256], P('head')
- o_weight_grad: float32 [1536, 1536], P('head', 'dp')
- gain_mlp_grad: float32 [1536], replicated
- gate_weight_grad: float32 [1536, 8960], P('dp', 'head')
- up_weight_grad: float32 [1536, 8960], P('dp', 'head')
- down_weight_grad: float32 [8960, 1536], P('head', 'dp')
Inputs may be any that keep to these rules, and one draw needn't show every extreme that they name: `row_lengths`: 3 document lengths that sum to 4096; the longest is exactly 2048. `source_weights`: numerators over the denominator 16.
All inputs are finite; a program needn't handle non-finite values.
Results may differ from a plain program's by a relative error of at most 0.025.
Values may be sent and summed in bfloat16 or wider, within the bound.
A program may use at most 256 MiB of HBM per device.

v0:
```python
import jax
import jax.numpy as jnp
from jax import lax
from jax.sharding import PartitionSpec as P

HEAD_SIZE = 128
BLOCK_TOKENS = 512


norm_epsilon = 1e-06
rope_base = 1000000.0
loss_denominator = 16.0
masked_score = -1e30


def doc_layout(row_lengths, first_token, token_count):
    doc_ends = jnp.cumsum(row_lengths)
    doc_starts = doc_ends - row_lengths
    token_index = first_token + jnp.arange(token_count, dtype=jnp.int32)
    doc_id = jnp.sum((doc_ends[None, :] <= token_index[:, None]).astype(jnp.int32), axis=1)
    doc_begin = jnp.max(
        jnp.where(doc_starts[None, :] <= token_index[:, None], doc_starts[None, :], 0), axis=1
    )
    return (doc_id, token_index - doc_begin, token_index)


def rope_tables(positions):
    freq = rope_base ** (-jnp.arange(0, HEAD_SIZE, 2, dtype=jnp.float32) / HEAD_SIZE)
    angle = positions.astype(jnp.float32)[:, None] * freq[None, :]
    angle = jnp.concatenate([angle, angle], axis=1)
    return (jnp.cos(angle)[:, None, :], jnp.sin(angle)[:, None, :])


def rotary_apply(values, cosine_table, sine_table):
    half_width = values.shape[-1] // 2
    turned = jnp.concatenate([-values[..., half_width:], values[..., :half_width]], axis=-1)
    return values * cosine_table + turned * sine_table


def unrotate(grads, cosine_table, sine_table):
    half_width = grads.shape[-1] // 2
    scaled_grad = grads * sine_table
    back_part = jnp.concatenate(
        [scaled_grad[..., half_width:], -scaled_grad[..., :half_width]], axis=-1
    )
    return grads * cosine_table + back_part


def rms_scale(values):
    return lax.rsqrt(jnp.mean(values * values, axis=-1, keepdims=True) + norm_epsilon)


def norm_back(grad_out, inputs, scale, gain):
    weighted = grad_out * gain
    return scale * weighted - inputs * scale**3 * jnp.mean(
        weighted * inputs, axis=-1, keepdims=True
    )


def body(
    layer_in,
    gain_attn,
    q_weight,
    q_bias,
    key_weight,
    key_bias,
    value_weight,
    value_bias,
    o_weight,
    gain_mlp,
    gate_weight,
    up_weight,
    down_weight,
    row_lengths,
    source_ids,
    source_weights,
    out_grad,
):
    tok_rows = layer_in.shape[0]
    first_token = lax.axis_index("dp") * tok_rows
    doc_id, positions, token_index = doc_layout(row_lengths, first_token, tok_rows)
    cosine_table, sine_table = rope_tables(positions)
    full_q, full_k, full_v, full_o = (
        lax.all_gather(q_weight, "dp", axis=0, tiled=True),
        lax.all_gather(key_weight, "dp", axis=0, tiled=True),
        lax.all_gather(value_weight, "dp", axis=0, tiled=True),
        lax.all_gather(o_weight, "dp", axis=1, tiled=True),
    )
    full_gate, full_up, full_down = (
        lax.all_gather(gate_weight, "dp", axis=0, tiled=True),
        lax.all_gather(up_weight, "dp", axis=0, tiled=True),
        lax.all_gather(down_weight, "dp", axis=1, tiled=True),
    )
    inputs = layer_in.astype(jnp.float32)
    scale_one = rms_scale(inputs)
    gain_one = gain_attn.astype(jnp.float32)
    normed = (inputs * scale_one * gain_one).astype(jnp.bfloat16)
    head_count = full_q.shape[1] // HEAD_SIZE
    query_pre = jnp.dot(normed, full_q, preferred_element_type=jnp.float32) + q_bias.astype(
        jnp.float32
    )
    key_unrotated = jnp.dot(normed, full_k, preferred_element_type=jnp.float32) + key_bias.astype(
        jnp.float32
    )
    value_matrix = (
        jnp.dot(normed, full_v, preferred_element_type=jnp.float32) + value_bias.astype(jnp.float32)
    ).astype(jnp.bfloat16)
    query_rows = rotary_apply(
        query_pre.reshape(tok_rows, head_count, HEAD_SIZE), cosine_table, sine_table
    ).astype(jnp.bfloat16)
    key_matrix = (
        rotary_apply(key_unrotated.reshape(tok_rows, 1, HEAD_SIZE), cosine_table, sine_table)
        .reshape(tok_rows, HEAD_SIZE)
        .astype(jnp.bfloat16)
    )
    key_all, value_all = (
        lax.all_gather(key_matrix, "dp", axis=0, tiled=True),
        lax.all_gather(value_matrix, "dp", axis=0, tiled=True),
    )
    doc_first = first_token - positions[0]
    low_block = doc_first // BLOCK_TOKENS
    high_block = (first_token + tok_rows - 1) // BLOCK_TOKENS + 1
    score_scale = HEAD_SIZE ** (-0.5)

    def block_scores(block_id, key_source, value_source):
        block_start = block_id * BLOCK_TOKENS
        key_block = lax.dynamic_slice_in_dim(key_source, block_start, BLOCK_TOKENS, 0)
        value_block = lax.dynamic_slice_in_dim(value_source, block_start, BLOCK_TOKENS, 0)
        key_doc, unused_pos, key_index = doc_layout(row_lengths, block_start, BLOCK_TOKENS)
        visible = (key_doc[None, :] == doc_id[:, None]) & (
            key_index[None, :] <= token_index[:, None]
        )
        scores = (
            jnp.einsum("thd,kd->thk", query_rows, key_block, preferred_element_type=jnp.float32)
            * score_scale
        )
        return (scores, visible[:, None, :], key_block, value_block, block_start)

    def stats_step(block_id, state_pair):
        row_max, row_mass = state_pair
        scores, visible, key_block, value_block, local_start = block_scores(
            block_id, key_all, value_all
        )
        scores = jnp.where(visible, scores, masked_score)
        new_max = jnp.maximum(row_max, jnp.max(scores, axis=2))
        row_mass = row_mass * jnp.exp(row_max - new_max) + jnp.sum(
            jnp.exp(scores - new_max[..., None]), axis=2
        )
        return (new_max, row_mass)

    start_max = jnp.full((tok_rows, head_count), masked_score, jnp.float32)
    start_mass = jnp.zeros((tok_rows, head_count), jnp.float32)
    row_max, row_mass = lax.fori_loop(low_block, high_block, stats_step, (start_max, start_mass))
    row_lse = row_max + jnp.log(row_mass)

    def output_step(block_id, running):
        scores, visible, key_block, value_block, local_start = block_scores(
            block_id, key_all, value_all
        )
        probs = jnp.where(visible, jnp.exp(scores - row_lse[..., None]), 0.0).astype(jnp.bfloat16)
        return running + jnp.einsum(
            "thk,kd->thd", probs, value_block, preferred_element_type=jnp.float32
        )

    attended_raw = lax.fori_loop(
        low_block,
        high_block,
        output_step,
        jnp.zeros((tok_rows, head_count, HEAD_SIZE), jnp.float32),
    )
    attended = attended_raw.reshape(tok_rows, head_count * HEAD_SIZE).astype(jnp.bfloat16)
    branch_part = jnp.dot(attended, full_o, preferred_element_type=jnp.float32)
    branch = lax.psum(branch_part.astype(jnp.bfloat16), "head").astype(jnp.float32)
    hidden = inputs + branch
    scale_two = rms_scale(hidden)
    gain_two = gain_mlp.astype(jnp.float32)
    normed_mlp = (hidden * scale_two * gain_two).astype(jnp.bfloat16)
    gate_act = jnp.dot(normed_mlp, full_gate, preferred_element_type=jnp.float32)
    up_act = jnp.dot(normed_mlp, full_up, preferred_element_type=jnp.float32)
    sigmoid_gate = jax.nn.sigmoid(gate_act)
    silu_gate = gate_act * sigmoid_gate
    active = (silu_gate * up_act).astype(jnp.bfloat16)
    mlp_part = jnp.dot(active, full_down, preferred_element_type=jnp.float32)
    mlp_out = lax.psum(mlp_part.astype(jnp.bfloat16), "head").astype(jnp.float32)
    layer_out = (hidden + mlp_out).astype(jnp.bfloat16)
    picked = source_ids[:, None] == jnp.arange(source_weights.shape[0], dtype=jnp.int32)[None, :]
    row_scale = (
        jnp.sum(jnp.where(picked, source_weights[None, :], 0), axis=1).astype(jnp.float32)
        / loss_denominator
    )
    cotangent = out_grad.astype(jnp.float32) * row_scale[:, None]
    mlp_grad = cotangent.astype(jnp.bfloat16)
    down_grad = jnp.einsum("tf,td->fd", active, mlp_grad, preferred_element_type=jnp.float32)
    d_active = jnp.einsum("td,fd->tf", mlp_grad, full_down, preferred_element_type=jnp.float32)
    d_gate = (d_active * up_act * sigmoid_gate * (1.0 + gate_act * (1.0 - sigmoid_gate))).astype(
        jnp.bfloat16
    )
    d_up = (d_active * silu_gate).astype(jnp.bfloat16)
    gate_grad = jnp.einsum("td,tf->df", normed_mlp, d_gate, preferred_element_type=jnp.float32)
    up_grad = jnp.einsum("td,tf->df", normed_mlp, d_up, preferred_element_type=jnp.float32)
    mlp_parts = (gate_grad, up_grad, down_grad)
    norm_two_part = jnp.einsum(
        "tf,df->td", d_gate, full_gate, preferred_element_type=jnp.float32
    ) + jnp.einsum("tf,df->td", d_up, full_up, preferred_element_type=jnp.float32)
    d_normed_mlp = lax.psum(norm_two_part.astype(jnp.bfloat16), "head").astype(jnp.float32)
    gain_two_local = jnp.sum(d_normed_mlp * hidden * scale_two, axis=0)
    d_hidden = cotangent + norm_back(d_normed_mlp, hidden, scale_two, gain_two)
    branch_grad = d_hidden.astype(jnp.bfloat16)
    out_proj_grad = jnp.einsum(
        "tc,td->cd", attended, branch_grad, preferred_element_type=jnp.float32
    )
    d_attended = jnp.einsum(
        "td,cd->tc", branch_grad, full_o, preferred_element_type=jnp.float32
    ).astype(jnp.bfloat16)
    d_heads = d_attended.reshape(tok_rows, head_count, HEAD_SIZE)
    row_delta = jnp.sum(d_heads.astype(jnp.float32) * attended_raw, axis=-1)
    key_back, value_back = (
        lax.all_gather(key_matrix, "dp", axis=0, tiled=True),
        lax.all_gather(value_matrix, "dp", axis=0, tiled=True),
    )

    def back_step(block_id, state_triple):
        d_query, d_keys, d_values = state_triple
        scores, visible, key_block, value_block, local_start = block_scores(
            block_id, key_back, value_back
        )
        probs = jnp.where(visible, jnp.exp(scores - row_lse[..., None]), 0.0)
        d_probs = jnp.einsum(
            "thd,kd->thk", d_heads, value_block, preferred_element_type=jnp.float32
        )
        d_scores = (probs * (d_probs - row_delta[..., None])).astype(jnp.bfloat16)
        d_query = d_query + jnp.einsum(
            "thk,kd->thd", d_scores, key_block, preferred_element_type=jnp.float32
        )
        key_term = jnp.einsum(
            "thk,thd->kd", d_scores, query_rows, preferred_element_type=jnp.float32
        )
        value_term = jnp.einsum(
            "thk,thd->kd", probs.astype(jnp.bfloat16), d_heads, preferred_element_type=jnp.float32
        )
        d_keys = lax.dynamic_update_slice_in_dim(
            d_keys,
            lax.dynamic_slice_in_dim(d_keys, local_start, BLOCK_TOKENS, 0) + key_term,
            local_start,
            0,
        )
        d_values = lax.dynamic_update_slice_in_dim(
            d_values,
            lax.dynamic_slice_in_dim(d_values, local_start, BLOCK_TOKENS, 0) + value_term,
            local_start,
            0,
        )
        return (d_query, d_keys, d_values)

    all_tokens = key_back.shape[0]
    start_triple = (
        jnp.zeros((tok_rows, head_count, HEAD_SIZE), jnp.float32),
        jnp.zeros((all_tokens, HEAD_SIZE), jnp.float32),
        jnp.zeros((all_tokens, HEAD_SIZE), jnp.float32),
    )
    d_query, d_keys, d_values = lax.fori_loop(low_block, high_block, back_step, start_triple)
    key_sums, value_sums = (
        lax.psum_scatter(d_keys, "dp", scatter_dimension=0, tiled=True),
        lax.psum_scatter(d_values, "dp", scatter_dimension=0, tiled=True),
    )
    d_queries = (d_query * score_scale).astype(jnp.bfloat16)
    d_key_rot = (key_sums * score_scale).astype(jnp.bfloat16)
    d_value_rows = value_sums.astype(jnp.bfloat16)
    d_query_pre = (
        unrotate(d_queries.astype(jnp.float32), cosine_table, sine_table)
        .reshape(tok_rows, head_count * HEAD_SIZE)
        .astype(jnp.bfloat16)
    )
    d_key_pre = (
        unrotate(
            d_key_rot.astype(jnp.float32).reshape(tok_rows, 1, HEAD_SIZE), cosine_table, sine_table
        )
        .reshape(tok_rows, HEAD_SIZE)
        .astype(jnp.bfloat16)
    )
    query_bias_local = jnp.sum(d_query_pre.astype(jnp.float32), axis=0)
    key_bias_local = jnp.sum(d_key_pre.astype(jnp.float32), axis=0)
    value_bias_local = jnp.sum(d_value_rows.astype(jnp.float32), axis=0)
    query_grad = jnp.einsum("td,tc->dc", normed, d_query_pre, preferred_element_type=jnp.float32)
    key_grad = jnp.einsum("td,tc->dc", normed, d_key_pre, preferred_element_type=jnp.float32)
    value_grad = jnp.einsum("td,tc->dc", normed, d_value_rows, preferred_element_type=jnp.float32)
    norm_one_part = jnp.einsum("tc,dc->td", d_query_pre, full_q, preferred_element_type=jnp.float32)
    norm_one_part = norm_one_part + jnp.einsum(
        "tc,dc->td", d_key_pre, full_k, preferred_element_type=jnp.float32
    )
    norm_one_part = norm_one_part + jnp.einsum(
        "tc,dc->td", d_value_rows, full_v, preferred_element_type=jnp.float32
    )
    d_normed = lax.psum(norm_one_part.astype(jnp.bfloat16), "head").astype(jnp.float32)
    gain_one_local = jnp.sum(d_normed * inputs * scale_one, axis=0)
    layer_in_grad = (d_hidden + norm_back(d_normed, inputs, scale_one, gain_one)).astype(
        jnp.bfloat16
    )
    q_part, k_part, v_part, o_part, gate_part, up_part, down_part = (
        lax.psum_scatter(query_grad, "dp", scatter_dimension=0, tiled=True),
        lax.psum_scatter(key_grad, "dp", scatter_dimension=0, tiled=True),
        lax.psum_scatter(value_grad, "dp", scatter_dimension=0, tiled=True),
        lax.psum_scatter(out_proj_grad, "dp", scatter_dimension=1, tiled=True),
        lax.psum_scatter(mlp_parts[0], "dp", scatter_dimension=0, tiled=True),
        lax.psum_scatter(mlp_parts[1], "dp", scatter_dimension=0, tiled=True),
        lax.psum_scatter(mlp_parts[2], "dp", scatter_dimension=1, tiled=True),
    )
    q_bias_sum, k_bias_sum, v_bias_sum, gain_one_sum, gain_two_sum = lax.psum(
        (query_bias_local, key_bias_local, value_bias_local, gain_one_local, gain_two_local), "dp"
    )
    return (
        layer_out,
        layer_in_grad,
        gain_one_sum,
        q_part,
        q_bias_sum,
        k_part,
        k_bias_sum,
        v_part,
        v_bias_sum,
        o_part,
        gain_two_sum,
        gate_part,
        up_part,
        down_part,
    )


def solution(mesh):
    placed = (
        P("dp", None),
        P(),
        P("dp", "head"),
        P("head"),
        P("dp", "head"),
        P("head"),
        P("dp", "head"),
        P("head"),
        P("head", "dp"),
        P(),
        P("dp", "head"),
        P("dp", "head"),
        P("head", "dp"),
        P(),
        P("dp"),
        P(),
        P("dp", None),
    )
    return jax.shard_map(
        body,
        mesh=mesh,
        in_specs=placed,
        out_specs=(
            P("dp", None),
            P("dp", None),
            P(),
            P("dp", "head"),
            P("head"),
            P("dp", "head"),
            P("head"),
            P("dp", "head"),
            P("head"),
            P("head", "dp"),
            P(),
            P("dp", "head"),
            P("dp", "head"),
            P("head", "dp"),
        ),
        check_vma=False,
    )
```

profile of v0, /device:TPU:1, one launch (start us, length us, event | category | flops | bytes accessed | tf_op | source)
XLA Modules:
  0.0 1976.2 jit_solution(12952017771399439875)
XLA Ops:
  8.8 24.3 %all_gather.29 = bf16[1536,128]{1,0:T(8,128)(2,1)S(1)} all-gather(bf16[96,128]{1,0:T(8,128)(2,1)} %param.27), channel_id=1, replica_groups=mesh['dp'=16,'head'=2] {'dp'}, dimensions={0}, use_global_device_ids=true | all-gather | bytes 417792 | tf_op jit(solution)/shard_map/all_gather | solution.py:85
  34.5 1.4 fusion.65
  36.4 1.7 convolution_add_fusion.6
  40.8 18.7 all_gather.32
  63.4 11.2 all-gather.8.cloned.1.call-done
  74.6 1.6 copy.63
  76.2 42.6 %all-gather.10.cloned.1.call-done = bf16[1536,768]{1,0:T(8,128)(2,1)} async-done(((bf16[96,768]{1,0:T(8,128)(2,1)}), bf16[1536,768]{1,0:T(8,128)(2,1)}) %all-gather.10.cloned.1.call-update) | async-done | bytes 2359312 | tf_op jit(solution)/shard_map/all_gather | solution.py:84
  118.8 3.4 convolution_add_fusion.4
  122.2 1.4 copy.60
  124.1 1.7 while.45
  125.8 32.3 %all-gather.12.cloned.1.call-done = bf16[4096,128]{1,0:T(8,128)(2,1)} async-done(((bf16[256,128]{1,0:T(8,128)(2,1)}), bf16[4096,128]{1,0:T(8,128)(2,1)}) %all-gather.12.cloned.1.call-update) | async-done | bytes 1048592 | tf_op jit(solution)/shard_map/all_gather | solution.py:118
  159.1 3.6 while.46
  159.4 3.3 fusion.182
  163.3 1.4 copy.65
  164.8 36.9 %all-gather.14.cloned.1.call-done = bf16[768,1536]{0,1:T(8,128)(2,1)} async-done(((bf16[768,96]{0,1:T(8,128)(2,1)}), bf16[768,1536]{0,1:T(8,128)(2,1)}) %all-gather.14.cloned.1.call-update) | async-done | bytes 2359312 | tf_op jit(solution)/shard_map/all_gather | solution.py:87
  201.6 3.4 convolution_convert_fusion.1
  207.8 30.0 %all-reduce.6.cloned.1.call-done = bf16[256,1536]{1,0:T(8,128)(2,1)} async-done(((bf16[256,1536]{1,0:T(8,128)(2,1)}), bf16[256,1536]{1,0:T(8,128)(2,1)}) %all-reduce.6.cloned.1.call-update) | async-done | bytes 786448 | tf_op jit(solution)/shard_map/psum | solution.py:173
  237.7 1.5 multiply_reduce_fusion
  239.3 1.2 multiply_convert_fusion.3
  240.5 107.7 %all-gather.16.cloned.1.call-done = bf16[1536,4480]{1,0:T(8,128)(2,1)} async-done(((bf16[96,4480]{1,0:T(8,128)(2,1)}), bf16[1536,4480]{1,0:T(8,128)(2,1)}) %all-gather.16.cloned.1.call-update) | async-done | bytes 13762576 | tf_op jit(solution)/shard_map/all_gather | solution.py:90
  348.2 11.1 fusion.113
  359.2 97.1 %all-gather.18.cloned.1.call-done = bf16[1536,4480]{1,0:T(8,128)(2,1)} async-done(((bf16[96,4480]{1,0:T(8,128)(2,1)}), bf16[1536,4480]{1,0:T(8,128)(2,1)}) %all-gather.18.cloned.1.call-update) | async-done | bytes 13762576 | tf_op jit(solution)/shard_map/all_gather | solution.py:91
  456.4 11.1 fusion.114
  467.5 97.1 %all-gather.20.cloned.1.call-done = bf16[4480,1536]{0,1:T(8,128)(2,1)} async-done(((bf16[4480,96]{0,1:T(8,128)(2,1)}), bf16[4480,1536]{0,1:T(8,128)(2,1)}) %all-gather.20.cloned.1.call-update) | async-done | bytes 13762576 | tf_op jit(solution)/shard_map/all_gather | solution.py:92
  564.5 14.0 multiply_convert_fusion
  578.6 9.9 fusion.115
  588.5 8.6 fusion.52
  597.2 32.1 %all-reduce.8.cloned.1.call-done = bf16[256,1536]{1,0:T(8,128)(2,1)} async-done(((bf16[256,1536]{1,0:T(8,128)(2,1)}), bf16[256,1536]{1,0:T(8,128)(2,1)}) %all-reduce.8.cloned.1.call-update) | async-done | bytes 786448 | tf_op jit(solution)/shard_map/psum | solution.py:205
  629.3 2.4 fusion.64
  632.3 3.7 convolution_convert_fusion.2
  635.9 1.2 copy.66
  638.9 1.6 broadcast.293.clone
  640.4 1.5 broadcast.293
  641.9 16.2 while.47
  643.2 2.1 fusion.194
  645.3 1.6 convolution_add_fusion.8
  647.0 1.7 constant_dynamic-slice_fusion.2
  648.7 1.8 copy.90
  650.4 2.2 fusion.195
  654.5 3.6 fusion.196
  659.1 10.3 convolution_convert_fusion
  673.0 92.2 %reduce-scatter.10.cloned.1.call-done = f32[256,128]{0,1:T(8,128)} async-done(((f32[4096,128]{0,1:T(8,128)}), f32[256,128]{0,1:T(8,128)}) %reduce-scatter.10.cloned.1.call-update) | async-done | bytes 131088 | tf_op jit(solution)/shard_map/reduce_scatter | solution.py:263
  765.1 1.3 fusion.87
  766.5 1.9 convert_reduce_fusion.5
  769.1 1.5 convolution_add_fusion.2
  770.6 59.0 %reduce-scatter.12.cloned.1.call-done = f32[256,128]{1,0:T(8,128)} async-done(((f32[4096,128]{1,0:T(8,128)}), f32[256,128]{1,0:T(8,128)}) %reduce-scatter.12.cloned.1.call-update) | async-done | bytes 131088 | tf_op jit(solution)/shard_map/reduce_scatter | solution.py:264
  829.6 2.8 fusion.53
  832.5 1.5 fusion.99
  834.0 1.4 fusion.95
  835.5 3.0 fusion.101
  838.6 1.2 copy-done.3
  840.6 4.1 fusion.78
  845.1 15.1 fusion.117
  860.3 15.3 fusion.118
  876.2 12.8 fusion.81
  890.1 1.6 fusion.71
  891.7 55.0 %all-reduce = (f32[1536]{0:T(1024)}, f32[768]{0:T(1024)}, f32[128]{0:T(128)}, f32[128]{0:T(128)}, f32[1536]{0:T(1024)}) all-reduce(f32[1536]{0:T(1024)S(1)} %get-tuple-element.592, f32[768]{0:T(1024)S(1)} %bitcast.185, f32[128]{0:T(128)S(1)} %copy-done.54, ...), channel_id=1, replica_groups=mesh['dp'=16,'head'=2] {'dp'}, use_global_device_ids=true, to_apply=%region_28.29 | all-reduce | flops 4096 | bytes 32768 | tf_op jit(solution)/shard_map/psum | solution.py:308
  946.8 3.8 fusion.59
  950.6 53.3 %reduce-scatter.18.cloned.1.call-done = f32[96,128]{1,0:T(8,128)} async-done(((f32[1536,128]{1,0:T(8,128)}), f32[96,128]{1,0:T(8,128)}) %reduce-scatter.18.cloned.1.call-update) | async-done | bytes 49168 | tf_op jit(solution)/shard_map/reduce_scatter | solution.py:302
  1003.9 79.1 %reduce-scatter.14.cloned.1.call-done = f32[96,768]{1,0:T(8,128)} async-done(((f32[1536,768]{1,0:T(8,128)}), f32[96,768]{1,0:T(8,128)}) %reduce-scatter.14.cloned.1.call-update) | async-done | bytes 294928 | tf_op jit(solution)/shard_map/reduce_scatter | solution.py:300
  1083.0 79.1 %reduce-scatter.20.cloned.1.call-done = f32[768,96]{0,1:T(8,128)} async-done(((f32[768,1536]{0,1:T(8,128)}), f32[768,96]{0,1:T(8,128)}) %reduce-scatter.20.cloned.1.call-update) | async-done | bytes 294928 | tf_op jit(solution)/shard_map/reduce_scatter | solution.py:303
  1162.0 270.2 %reduce-scatter.22.cloned.1.call-done = f32[96,4480]{1,0:T(8,128)} async-done(((f32[1536,4480]{1,0:T(8,128)}), f32[96,4480]{1,0:T(8,128)}) %reduce-scatter.22.cloned.1.call-update) | async-done | bytes 1720336 | tf_op jit(solution)/shard_map/reduce_scatter | solution.py:304
  1432.2 268.4 %reduce-scatter.24.cloned.1.call-done = f32[96,4480]{1,0:T(8,128)} async-done(((f32[1536,4480]{1,0:T(8,128)}), f32[96,4480]{1,0:T(8,128)}) %reduce-scatter.24.cloned.1.call-update) | async-done | bytes 1720336 | tf_op jit(solution)/shard_map/reduce_scatter | solution.py:305
  1700.6 268.6 %reduce-scatter.26.cloned.1.call-done = f32[4480,96]{0,1:T(8,128)} async-done(((f32[4480,1536]{0,1:T(8,128)}), f32[4480,96]{0,1:T(8,128)}) %reduce-scatter.26.cloned.1.call-update) | async-done | bytes 1720336 | tf_op jit(solution)/shard_map/reduce_scatter | solution.py:306
  (220 shorter events, 29.5 us)
Async XLA Ops:
  7.2 67.4 %all-gather.8.cloned.1.call-start = ((), (), s32[]{:S(2)}) async-start(), calls=%async_computation.9 | async-start | bytes 1114112 | tf_op jit(solution)/shard_map/all_gather | solution.py:117
  33.1 6.9 copy-start.18
  35.8 5.0 copy-start.58
  35.8 5.0 copy-start.41
  36.4 82.4 %copy-start.35 = (f32[256]{0:T(256)}, f32[256]{0:T(256)S(1)}, u32[]{:S(2)}) copy-start(f32[256]{0:T(256)S(1)} %get-tuple-element.694) | copy-start | bytes 3076
  36.4 23.9 %copy-start = (bf16[256,1536]{1,0:T(8,128)(2,1)S(1)}, bf16[256,1536]{1,0:T(8,128)(2,1)}, u32[]{:S(2)}) copy-start(bf16[256,1536]{1,0:T(8,128)(2,1)} %param.23) | copy-start | bytes 2359300
  40.0 83.7 %copy-start.22 = (f32[256,128]{0,1:T(8,128)}, f32[256,128]{0,1:T(8,128)S(1)}, u32[]{:S(2)}) copy-start(f32[256,128]{0,1:T(8,128)S(1)} %get-tuple-element.690) | copy-start | bytes 393220
  40.0 83.7 %copy-start.26 = (f32[256,128]{0,1:T(8,128)}, f32[256,128]{0,1:T(8,128)S(1)}, u32[]{:S(2)}) copy-start(f32[256,128]{0,1:T(8,128)S(1)} %get-tuple-element.692) | copy-start | bytes 393220
  40.0 23.3 %copy-start.59 = (s32[3]{0:T(128)S(1)}, s32[3]{0:T(128)}, u32[]{:S(2)}) copy-start(s32[3]{0:T(128)} %param.36) | copy-start | bytes 40
  40.0 23.4 %copy-start.55 = (bf16[768]{0:T(1024)(128)(2,1)S(1)}, bf16[768]{0:T(1024)(128)(2,1)}, u32[]{:S(2)}) copy-start(bf16[768]{0:T(1024)(128)(2,1)} %param.26) | copy-start | bytes 4612
  40.0 78.8 %all-gather.10.cloned.1.call-start = ((), (), s32[]{:S(2)}) async-start(), calls=%async_computation.10 | async-start | bytes 2506752 | tf_op jit(solution)/shard_map/all_gather | solution.py:84
  40.8 117.4 %all-gather.12.cloned.1.call-start = ((), (), s32[]{:S(2)}) async-start(), calls=%async_computation.11 | async-start | bytes 1114112 | tf_op jit(solution)/shard_map/all_gather | solution.py:118
  61.4 140.2 %all-gather.14.cloned.1.call-start = ((), (), s32[]{:S(2)}) async-start(), calls=%async_computation.12 | async-start | bytes 2506752 | tf_op jit(solution)/shard_map/all_gather | solution.py:87
  62.0 175.7 %all-reduce.6.cloned.1.call-start = ((), (), s32[]{:S(2)}) async-start(), calls=%async_computation.13 | async-start | bytes 1572864 | tf_op jit(solution)/shard_map/psum | solution.py:173
  164.7 40.3 %copy-start.6 = (f32[256,6,128]{0,2,1:T(8,128)}, f32[256,6,128]{0,2,1:T(8,128)S(1)}, u32[]{:S(2)}) copy-start(f32[256,6,128]{0,2,1:T(8,128)S(1)} %copy.65) | copy-start | bytes 2359300
  164.7 40.2 %copy-start.16 = (bf16[256,6,128]{0,2,1:T(8,128)(2,1)}, bf16[256,6,128]{0,2,1:T(8,128)(2,1)S(1)}, u32[]{:S(2)}) copy-start(bf16[256,6,128]{0,2,1:T(8,128)(2,1)S(1)} %convert_element_type.186) | copy-start | bytes 1179652
  205.0 2.6 copy-start.52
  205.0 2.7 copy-start.56
  205.0 2.7 copy-start.57
  205.0 143.1 %all-gather.16.cloned.1.call-start = ((), (), s32[]{:S(2)}) async-start(), calls=%async_computation.14 | async-start | bytes 14622720 | tf_op jit(solution)/shard_map/all_gather | solution.py:90
  205.6 250.7 %all-gather.18.cloned.1.call-start = ((), (), s32[]{:S(2)}) async-start(), calls=%async_computation.15 | async-start | bytes 14622720 | tf_op jit(solution)/shard_map/all_gather | solution.py:91
  206.4 358.2 %all-gather.20.cloned.1.call-start = ((), (), s32[]{:S(2)}) async-start(), calls=%async_computation.16 | async-start | bytes 14622720 | tf_op jit(solution)/shard_map/all_gather | solution.py:92
  207.1 422.2 %all-reduce.8.cloned.1.call-start = ((), (), s32[]{:S(2)}) async-start(), calls=%async_computation.17 | async-start | bytes 1572864 | tf_op jit(solution)/shard_map/psum | solution.py:205
  207.7 424.0 %copy-start.33 = (f32[1536]{0:T(1024)}, f32[1536]{0:T(1024)S(1)}, u32[]{:S(2)}) copy-start(f32[1536]{0:T(1024)S(1)} %convert_element_type.190) | copy-start | bytes 18436
  207.8 423.9 %copy-start.43 = (f32[256]{0:T(256)}, f32[256]{0:T(256)S(1)}, u32[]{:S(2)}) copy-start(f32[256]{0:T(256)S(1)} %convert_multiply_fusion.13) | copy-start | bytes 3076
  237.7 1.6 copy-start.2
  239.3 392.4 %copy-start.39 = (f32[256]{0:T(256)}, f32[256]{0:T(256)S(1)}, u32[]{:S(2)}) copy-start(f32[256]{0:T(256)S(1)} %get-tuple-element.696) | copy-start | bytes 3076
  239.3 392.4 %copy-start.45 = (f32[256]{0:T(256)}, f32[256]{0:T(256)S(1)}, u32[]{:S(2)}) copy-start(f32[256]{0:T(256)S(1)} %get-tuple-element.695) | copy-start | bytes 3076
  578.6 9.9 copy-start.15
  578.6 9.9 copy-start.14
  597.2 168.0 %reduce-scatter.10.cloned.1.call-start = ((), (), s32[]{:S(2)}) async-start(), calls=%async_computation.18 | async-start | bytes 2228224 | tf_op jit(solution)/shard_map/reduce_scatter | solution.py:263
  629.3 3.0 copy-start.8
  629.3 3.0 copy-start.10
  635.9 2.2 copy-start.7
  642.9 2.5 copy-start.1
  643.2 2.2 copy-start.12
  654.5 3.6 copy-start.5
  658.1 171.5 %reduce-scatter.12.cloned.1.call-start = ((), (), s32[]{:S(2)}) async-start(), calls=%async_computation.19 | async-start | bytes 2228224 | tf_op jit(solution)/shard_map/reduce_scatter | solution.py:264
  658.9 231.2 %all-reduce.10.cloned.1.call-start = ((), (), s32[]{:S(2)}) async-start(), calls=%async_computation.27 | async-start | bytes 3145728 | tf_op jit(solution)/shard_map/psum | solution.py:184
  670.4 1.7 copy-start.13
  672.1 93.0 %copy-start.29 = (f32[256,64]{0,1:T(8,128)S(1)}, f32[256,64]{0,1:T(8,128)}, u32[]{:S(2)}) copy-start(f32[256,64]{0,1:T(8,128)} %copy-done.28) | copy-start | bytes 196612
  672.1 96.9 %copy-start.19 = (bf16[1536,128]{1,0:T(8,128)(2,1)S(1)}, bf16[1536,128]{1,0:T(8,128)(2,1)}, u32[]{:S(2)}) copy-start(bf16[1536,128]{1,0:T(8,128)(2,1)} %copy-done.18) | copy-start | bytes 1179652
  769.1 60.5 %copy-start.21 = (bf16[1536,128]{1,0:T(8,128)(2,1)S(1)}, bf16[1536,128]{1,0:T(8,128)(2,1)}, u32[]{:S(2)}) copy-start(bf16[1536,128]{1,0:T(8,128)(2,1)} %copy-done.20) | copy-start | bytes 1179652
  770.6 61.9 %copy-start.31 = (bf16[256,128]{0,1:T(8,128)(2,1)S(1)}, bf16[256,128]{0,1:T(8,128)(2,1)}, u32[]{:S(2)}) copy-start(bf16[256,128]{0,1:T(8,128)(2,1)} %copy-done.30) | copy-start | bytes 196612
  770.6 61.9 %copy-start.36 = (f32[256]{0:T(256)S(1)}, f32[256]{0:T(256)}, u32[]{:S(2)}) copy-start(f32[256]{0:T(256)} %copy-done.35) | copy-start | bytes 3076
  832.4 1.6 copy-start.24
  832.4 118.2 %reduce-scatter.16.cloned.1.call-start = ((), (), s32[]{:S(2)}) async-start(), calls=%async_computation.21 | async-start | bytes 835584 | tf_op jit(solution)/shard_map/reduce_scatter | solution.py:301
  834.0 169.9 %reduce-scatter.18.cloned.1.call-start = ((), (), s32[]{:S(2)}) async-start(), calls=%async_computation.22 | async-start | bytes 835584 | tf_op jit(solution)/shard_map/reduce_scatter | solution.py:302
  835.4 247.5 %reduce-scatter.14.cloned.1.call-start = ((), (), s32[]{:S(2)}) async-start(), calls=%async_computation.20 | async-start | bytes 5013504 | tf_op jit(solution)/shard_map/reduce_scatter | solution.py:300
  838.5 1.7 copy-start.9
  838.5 2.0 copy-start.11
  838.5 2.1 copy-start.17
  838.5 2.1 copy-start.34
  838.6 323.4 %reduce-scatter.20.cloned.1.call-start = ((), (), s32[]{:S(2)}) async-start(), calls=%async_computation.23 | async-start | bytes 5013504 | tf_op jit(solution)/shard_map/reduce_scatter | solution.py:303
  844.8 587.4 %reduce-scatter.22.cloned.1.call-start = ((), (), s32[]{:S(2)}) async-start(), calls=%async_computation.24 | async-start | bytes 29245440 | tf_op jit(solution)/shard_map/reduce_scatter | solution.py:304
  860.2 840.4 %reduce-scatter.24.cloned.1.call-start = ((), (), s32[]{:S(2)}) async-start(), calls=%async_computation.25 | async-start | bytes 29245440 | tf_op jit(solution)/shard_map/reduce_scatter | solution.py:305
  875.6 1093.6 %reduce-scatter.26.cloned.1.call-start = ((), (), s32[]{:S(2)}) async-start(), calls=%async_computation.26 | async-start | bytes 29245440 | tf_op jit(solution)/shard_map/reduce_scatter | solution.py:306
  890.0 1.7 copy-start.38
  890.0 1.7 copy-start.42
  890.0 1.7 copy-start.54
  890.0 56.8 %copy-start.40 = (f32[256]{0:T(256)S(1)}, f32[256]{0:T(256)}, u32[]{:S(2)}) copy-start(f32[256]{0:T(256)} %copy-done.39) | copy-start | bytes 3076
  890.0 56.8 %copy-start.46 = (f32[256]{0:T(256)S(1)}, f32[256]{0:T(256)}, u32[]{:S(2)}) copy-start(f32[256]{0:T(256)} %copy-done.45) | copy-start | bytes 3076
  890.0 56.8 %copy-start.48 = (f32[256]{0:T(256)S(1)}, f32[256]{0:T(256)}, u32[]{:S(2)}) copy-start(f32[256]{0:T(256)} %copy-done.47) | copy-start | bytes 3076
  890.0 56.8 %copy-start.53 = (f32[256]{0:T(256)S(1)}, f32[256]{0:T(256)}, u32[]{:S(2)}) copy-start(f32[256]{0:T(256)} %get-tuple-element.693) | copy-start | bytes 3076
  (15 other events, 13.7 us)
Sparse Core Ops, SparseCore 0:
  40.1 34.4 all-gather.7
  76.9 41.8 all-gather.9
  121.6 36.5 all-gather.11
  160.3 41.2 all-gather.13
  205.2 32.5 all-reduce.5
  239.9 108.2 all-gather.15
  350.5 105.8 all-gather.17
  458.7 105.8 all-gather.19
  597.3 31.9 all-reduce.7
  658.2 106.8 reduce-scatter.9
  768.9 60.6 reduce-scatter.11
  832.5 52.1 all-reduce.9
  888.9 55.3 reduce-scatter.15
  948.3 55.5 reduce-scatter.17
  1008.2 74.7 reduce-scatter.13
  1087.2 74.7 reduce-scatter.19
  1166.6 265.6 reduce-scatter.21
  1436.7 263.8 reduce-scatter.23
  1705.3 263.8 reduce-scatter.25
where the time goes:
time: 1990 us; the launch traced here: 1980 us
  waiting for transfers between devices  1660 us (83%)
  matrix products  151 us (8%)
  blocking collectives  98 us (5%)
  local copies, waits for them, and re-layouts  25.5 us (1%)
  other arithmetic  23.7 us (1%)
    reduce_scatter x1, waiting for transfers between devices, body(): lax.psum_scatter(mlp_parts[0], 'dp', scatter_dimension=0, tiled=True)  270 us
    reduce_scatter x1, waiting for transfers between devices, body(): lax.psum_scatter(mlp_parts[2], 'dp', scatter_dimension=1, tiled=True)  269 us
    reduce_scatter x1, waiting for transfers between devices, body(): lax.psum_scatter(mlp_parts[1], 'dp', scatter_dimension=0, tiled=True)  268 us
    all_gather x1, waiting for transfers between devices, body(): lax.all_gather(gate_weight, 'dp', axis=0, tiled=True)  108 us
    all_gather x1, waiting for transfers between devices, body(): lax.all_gather(up_weight, 'dp', axis=0, tiled=True)  97.1 us
    all_gather x1, waiting for transfers between devices, body(): lax.all_gather(down_weight, 'dp', axis=1, tiled=True)  97.1 us
    reduce_scatter x1, waiting for transfers between devices, body(): lax.psum_scatter(d_keys, 'dp', scatter_dimension=0, tiled=True)  92.2 us
    reduce_scatter x1, waiting for transfers between devices, body(): lax.psum_scatter(query_grad, 'dp', scatter_dimension=0, tiled=True)  79.1 us
  transfers between devices with their start and end apart: 19, of which 17 were waited for; matrix products, arithmetic and copies ran while one was open for 6% of the time, Pallas kernels for 0%

commit v1 on v0

v1 whole, which is shorter than its diff:
```python
import dataclasses
import functools
from typing import Any, Callable
import jax
import jax.numpy as jnp
from jax import lax
from jax.experimental import pallas as pl
from jax.experimental.pallas import tpu as pltpu
from jax.sharding import PartitionSpec as P

HEAD_SIZE = 128
KEYS = 256
SCALE = HEAD_SIZE**-0.5
SCALE2 = SCALE * 1.4426950408889634
MESH = pl.DeviceIdType.MESH
LANES = 128
norm_epsilon = 1e-06
rope_base = 1000000.0
loss_denominator = 16.0
masked_score = -1e30
VMEM = pl.BlockSpec(memory_space=pltpu.VMEM)
HBM = pl.BlockSpec(memory_space=pl.ANY)
dma = pltpu.SemaphoreType.DMA


def grid_of(count):
    across = 2 if count <= 16 else 4
    return count // (2 * across), across


def remote(src, dst, send, recv, where):
    return pltpu.make_async_remote_copy(
        src_ref=src, dst_ref=dst, send_sem=send, recv_sem=recv, device_id=where, device_id_type=MESH
    )


class Grid:
    def __init__(self, count, tower=False):
        self.lines, self.columns = grid_of(count)
        self.tower = tower
        self.across = 2 if tower else self.columns
        me, self.half = lax.axis_index("dp"), lax.axis_index("head")
        self.me = me
        self.core = me % 2
        self.column = (me // 2) % self.columns
        self.row = me // (2 * self.columns)
        self.col = self.half if tower else self.column

    def where(self, r, q, k):
        if self.tower:
            return {"dp": (r * self.columns + self.column) * 2 + k, "head": q}
        return {"dp": (r * self.columns + q) * 2 + k, "head": self.half}

    def index(self, r, q, k):
        return (r * self.across + q) * 2 + k


@dataclasses.dataclass
class Task:
    inputs: list
    in_specs: list
    outs: list
    out_specs: list
    scratch: list
    targets: Callable
    run: Callable
    pace: int = 1


def fuse(ident, name, *tasks):
    remote_ops = any(t.targets is not None for t in tasks)

    def split(refs, sizes):
        parts, start = [], 0
        for size in sizes:
            parts.append(refs[start : start + size])
            start += size
        return parts

    n_in = [len(t.inputs) for t in tasks]
    n_out = [len(t.outs) for t in tasks]
    n_scratch = [len(t.scratch) for t in tasks]

    def kernel(*refs):
        ins, outs, scratch = split(refs, [sum(n_in), sum(n_out), sum(n_scratch)])
        if remote_ops:
            barrier = pltpu.get_barrier_semaphore()
            known, total = set(), 0
            for t in tasks:
                for key, ok, where in t.targets() if t.targets is not None else ():
                    if key in known:
                        continue
                    known.add(key)
                    if ok is True:
                        pl.semaphore_signal(barrier, inc=1, device_id=where, device_id_type=MESH)
                        total = total + 1
                    else:

                        @pl.when(ok)
                        def _():
                            pl.semaphore_signal(barrier, inc=1, device_id=where, device_id_type=MESH)

                        total = total + ok.astype(jnp.int32)
            pl.semaphore_wait(barrier, total)
        live = [
            (t.run(*a, *b, *c), t.pace)
            for t, a, b, c in zip(tasks, split(ins, n_in), split(outs, n_out), split(scratch, n_scratch))
        ]
        while live:
            kept = []
            for steps, pace in live:
                for _ in range(pace):
                    if next(steps, None) is None:
                        break
                else:
                    kept.append((steps, pace))
            live = kept

    params = dict(vmem_limit_bytes=60 << 20)
    if remote_ops:
        params.update(collective_id=ident, has_side_effects=True)
    flat = pl.pallas_call(
        kernel,
        out_shape=[o for t in tasks for o in t.outs],
        in_specs=[s for t in tasks for s in t.in_specs],
        out_specs=[s for t in tasks for s in t.out_specs],
        scratch_shapes=[s for t in tasks for s in t.scratch],
        compiler_params=pltpu.CompilerParams(**params),
        name=name,
    )(*[x for t in tasks for x in t.inputs])
    return split(flat, n_out)


def gather(x, count, tower=False, pieces=1, both=False, pace=1):
    lines, columns = grid_of(count)
    across = 2 if tower else columns
    members = lines * across * 2
    shape = x.shape
    pieces = 1 if both else pieces
    x = x.reshape((pieces, shape[0] // pieces) + shape[1:])
    copies = 2 if both else pieces

    def hops_of(grid):
        row, col, core = grid.row, grid.col, grid.core
        return (
            (row < lines - 1, grid.where(row + 1, col, core)),
            (row > 0, grid.where(row - 1, col, core)),
            (col < across - 1, grid.where(row, col + 1, core)),
            (col > 0, grid.where(row, col - 1, core)),
            (True, grid.where(row, col, 1 - core)),
        )

    def targets():
        grid = Grid(count, tower)
        found = [(("hop", tower, i), ok, to) for i, (ok, to) in enumerate(hops_of(grid))]
        if both:
            found.append(("half", True, {"dp": grid.me, "head": 1 - grid.half}))
        return found

    def run(x_ref, o_ref, send, recv, local, cross):
        grid = Grid(count, tower)
        hops = hops_of(grid)
        core, col, row = grid.core, grid.col, grid.row
        me = grid.index(row, col, core)

        def copy(hop, shard, piece, src):
            return remote(src, o_ref.at[shard, piece], send.at[hop, shard, piece], recv.at[shard, piece], hops[hop][1])

        order = sorted(
            ((dr, dq) for dr in range(1 - lines, lines) for dq in range(1 - across, across)),
            key=lambda p: (abs(p[0]) + abs(p[1]), abs(p[1])),
        )
        if both:
            pair = remote(
                x_ref.at[0], o_ref.at[me, 1], cross.at[0], cross.at[1], {"dp": grid.me, "head": 1 - grid.half}
            )
            pair.start()
        sends = []
        mine = pltpu.make_async_copy(x_ref, o_ref.at[me, pl.ds(0, pieces)], local)
        for dr, dq in order:
            shard = grid.index(row - dr, col - dq, core)
            valid = (row - dr >= 0) & (row - dr < lines) & (col - dq >= 0) & (col - dq < across)
            onward = []
            if dq == 0:
                if dr >= 0:
                    onward.append(0)
                if dr <= 0:
                    onward.append(1)
            if dq >= 0:
                onward.append(2)
            if dq <= 0:
                onward.append(3)
            onward.append(4)
            for piece in range(copies):
                own = dr == 0 and dq == 0
                src = o_ref.at[shard, piece]
                if own and piece < pieces:
                    src = x_ref.at[piece]
                if own and piece >= pieces:
                    pair.wait_recv()
                if not own:

                    @pl.when(valid)
                    def _():
                        copy(4, shard, piece, src).wait_recv()

                for hop in onward:
                    ok = hops[hop][0]
                    go = valid if ok is True else valid & ok

                    @pl.when(go)
                    def _():
                        copy(hop, shard, piece, src).start()

                    sends.append((go, hop, shard, piece, src))
                yield True
            if dr == 0 and dq == 0:
                mine.start()
        for r in range(lines):
            for q in range(across):
                for piece in range(copies):
                    shard = grid.index(r, q, 1 - core)
                    copy(4, shard, piece, o_ref.at[shard, piece]).wait_recv()
        yield True
        for go, hop, shard, piece, src in sends:

            @pl.when(go)
            def _():
                copy(hop, shard, piece, src).wait_send()

        mine.wait()
        if both:
            pair.wait_send()

    return Task(
        [x],
        [VMEM],
        [jax.ShapeDtypeStruct((members, copies) + x.shape[1:], x.dtype)],
        [HBM],
        [dma((5, members, copies)), dma((members, copies)), dma, dma((2,))],
        targets,
        run,
        pace,
    )


def scatter(x, count, tower=False, dtype=jnp.float32, pace=1):
    lines, columns = grid_of(count)
    across = 2 if tower else columns
    members = lines * across * 2
    block = (x.shape[0] // members,) + x.shape[1:]
    height = block[0]
    step = 16
    x = x.reshape((members,) + block)

    def targets():
        grid = Grid(count, tower)
        row, col, core = grid.row, grid.col, grid.core
        found = [(("hop", tower, 4), True, grid.where(row, col, 1 - core))]
        found += [(("col", tower, e), True, grid.where(row, (col + e) % across, core)) for e in range(1, across)]
        found += [(("row", tower, d), True, grid.where((row + d) % lines, col, core)) for d in range(1, lines)]
        return found

    def run(x_ref, o_ref, near, first, wide, second, far, s1, r1, s2, r2, s3, r3):
        grid = Grid(count, tower)
        row, col, core = grid.row, grid.col, grid.core

        def one(r, q):
            return remote(
                x_ref.at[grid.index(r, q, 1 - core)], near.at[r, q], s1.at[r, q], r1.at[r, q], grid.where(row, col, 1 - core)
            )

        def two(r, e):
            return remote(
                first.at[r, e - 1], wide.at[r, e - 1], s2.at[r, e], r2.at[r, e], grid.where(row, (col + e) % across, core)
            )

        def three(d):
            return remote(
                second.at[d - 1], far.at[d - 1], s3.at[d], r3.at[d], grid.where((row + d) % lines, col, core)
            )

        lines_order = [d for d in range(1, lines)] + [0]
        for d in lines_order:
            r = (row + d) % lines
            for e in [e for e in range(1, across)] + [0]:
                one(r, (col + e) % across).start()
        yield True

        def blocks(body):
            def run_block(i, carry):
                body(pl.ds(pl.multiple_of(i * step, step), step))
                return carry

            lax.fori_loop(0, height // step, run_block, 0)

        for d in lines_order:
            r = (row + d) % lines
            for e in range(1, across):
                q = (col + e) % across
                one(r, q).wait_recv()

                def add(rows):
                    first[r, e - 1, rows] = (
                        x_ref[grid.index(r, q, core), rows].astype(jnp.float32) + near[r, q, rows].astype(jnp.float32)
                    ).astype(first.dtype)

                blocks(add)
                two(r, e).start()
            yield True
        for d in lines_order:
            r = (row + d) % lines
            one(r, col).wait_recv()
            for e in range(1, across):
                two(r, e).wait_recv()

            def total(rows):
                value = x_ref[grid.index(r, col, core), rows].astype(jnp.float32) + near[r, col, rows].astype(jnp.float32)
                for e in range(1, across):
                    value = value + wide[r, e - 1, rows].astype(jnp.float32)
                return value

            if d:

                def add(rows):
                    second[d - 1, rows] = total(rows).astype(second.dtype)

                blocks(add)
                three(d).start()
            else:
                for e in range(1, lines):
                    three(e).wait_recv()

                def add(rows):
                    value = total(rows)
                    for e in range(1, lines):
                        value = value + far[e - 1, rows].astype(jnp.float32)
                    o_ref[rows] = value.astype(o_ref.dtype)

                blocks(add)
            yield True
        for r in range(lines):
            for q in range(across):
                one(r, q).wait_send()
            for e in range(1, across):
                two(r, e).wait_send()
        for d in range(1, lines):
            three(d).wait_send()

    return Task(
        [x],
        [VMEM],
        [jax.ShapeDtypeStruct(block, dtype)],
        [VMEM],
        [
            pltpu.VMEM((lines, across) + block, x.dtype),
            pltpu.VMEM((lines, across - 1) + block, x.dtype),
            pltpu.VMEM((lines, across - 1) + block, x.dtype),
            pltpu.VMEM((lines - 1,) + block, x.dtype),
            pltpu.VMEM((lines - 1,) + block, x.dtype),
            dma((lines, across)),
            dma((lines, across)),
            dma((lines, across)),
            dma((lines, across)),
            dma((lines,)),
            dma((lines,)),
        ],
        targets,
        run,
        pace,
    )


def scatter_all(x, count, ident, name, **how):
    cuts = max(1, x.size * x.dtype.itemsize >> 23)
    span = x.shape[1] // cuts
    parts = [
        fuse(ident + i, f"{name}{i}", scatter(x[:, i * span : (i + 1) * span], count, **how))[0][0] for i in range(cuts)
    ]
    return parts[0] if cuts == 1 else jnp.concatenate(parts, axis=1)


def swap(arrays, pace=1):
    parts = len(arrays)

    def targets():
        return [("half", True, {"dp": lax.axis_index("dp"), "head": 1 - lax.axis_index("head")})]

    def run(*refs):
        ins, outs = refs[:parts], refs[parts : 2 * parts]
        send, recv = refs[2 * parts :]
        where = targets()[0][2]
        copies = [remote(ins[i], outs[i], send.at[i], recv.at[i], where) for i in range(parts)]
        for copy in copies:
            copy.start()
        yield True
        for copy in copies:
            copy.wait()

    return Task(
        list(arrays),
        [VMEM] * parts,
        [jax.ShapeDtypeStruct(a.shape, a.dtype) for a in arrays],
        [VMEM] * parts,
        [dma((parts,)), dma((parts,))],
        targets,
        run,
        pace,
    )


def unit_targets(count):
    lines, columns = grid_of(count)
    grid = Grid(count)
    mine = grid.row * 2 + grid.core
    found = []
    for e in range(1, 2 * lines):
        member = mine ^ e
        found.append((("member", e), True, grid.where(member // 2, grid.column, member % 2)))
    for e in range(1, columns):
        found.append((("col", False, e), True, grid.where(grid.row, (grid.column + e) % columns, grid.core)))
    return found


def spread(w, count, pace=1):
    lines, columns = grid_of(count)
    kinds, depth, width = w.shape
    tiles = width // LANES
    members = 2 * lines
    slots = pl.cdiv(tiles, members)
    twice = 2 * depth

    def run(w_ref, o_ref, zeros, send, recv, push, pull, blank):
        grid = Grid(count)
        mine = grid.row * 2 + grid.core

        def lanes(slot):
            return pl.ds(slot * LANES, LANES)

        def bytes_of(slot):
            return o_ref.at[:, pl.ds(0, members * depth), lanes(slot)]

        def full(slot, member):
            return True if (slot + 1) * members <= tiles else slot * members + member < tiles

        def guarded(ok, body):
            if ok is True:
                body()
            else:
                pl.when(ok)(body)

        def block(slot, member):
            return w_ref.at[:, :, pl.ds(pl.multiple_of((slot * members + member) * LANES, LANES), LANES)]

        def spot(slot):
            return o_ref.at[:, pl.ds(pl.multiple_of(grid.me * depth, depth), depth), lanes(slot)]

        def out(slot, e):
            member = mine ^ e
            return remote(
                block(slot, member),
                spot(slot),
                send.at[slot, e],
                recv.at[slot],
                grid.where(member // 2, grid.column, member % 2),
            )

        def chunk(slot, r, column):
            return o_ref.at[:, pl.ds(pl.multiple_of((r * columns + column) * twice, twice), twice), lanes(slot)]

        def over(slot, r, e):
            here = chunk(slot, r, grid.column)
            return remote(
                here,
                here,
                push.at[slot, r, e],
                pull.at[slot, e],
                grid.where(grid.row, (grid.column + e) % columns, grid.core),
            )

        for slot in range(slots):
            for e in range(1, members):
                guarded(full(slot, mine ^ e), lambda: out(slot, e).start())
            guarded(
                full(slot, mine), lambda: pltpu.make_async_copy(block(slot, mine), spot(slot), recv.at[slot]).start()
            )
        last = slots - 1
        some = full(last, mine)
        if some is not True:
            fills = [
                pltpu.make_async_copy(zeros, o_ref.at[:, pl.ds(i * depth, depth), lanes(last)], blank.at[i])
                for i in range(count)
            ]

            @pl.when(jnp.logical_not(some))
            def _():
                zeros[...] = jnp.zeros_like(zeros)
                for fill in fills:
                    fill.start()
                for fill in fills:
                    fill.wait()

        yield True
        for slot in range(slots):

            def pass_on():
                pltpu.make_async_copy(bytes_of(slot), bytes_of(slot), recv.at[slot]).wait()
                for r in range(lines):
                    for e in range(1, columns):
                        over(slot, r, e).start()

            guarded(full(slot, mine), pass_on)
            yield True
        for slot in range(slots):

            def finish():
                for e in range(1, columns):
                    pltpu.make_async_copy(bytes_of(slot), bytes_of(slot), pull.at[slot, e]).wait()
                    for r in range(lines):
                        over(slot, r, e).wait_send()

            guarded(full(slot, mine), finish)
            for e in range(1, members):
                guarded(full(slot, mine ^ e), lambda: out(slot, e).wait_send())

    return Task(
        [w],
        [VMEM],
        [jax.ShapeDtypeStruct((kinds, count * depth, slots * LANES), w.dtype)],
        [HBM],
        [
            pltpu.VMEM((kinds, depth, LANES), w.dtype),
            dma((slots, members)),
            dma((slots,)),
            dma((slots, lines, columns)),
            dma((slots, columns)),
            dma((count,)),
        ],
        functools.partial(unit_targets, count),
        run,
        pace,
    )


def collect(g, count, width, pace=1):
    lines, columns = grid_of(count)
    kinds, rows, span = g.shape
    tiles = width // LANES
    members = 2 * lines
    slots = span // LANES
    depth = rows // count
    twice = 2 * depth

    def run(g_ref, o_ref, near, stage, push, pull, send, recv):
        grid = Grid(count)
        mine = grid.row * 2 + grid.core

        def lanes(slot):
            return pl.ds(slot * LANES, LANES)

        def guarded(slot, body):
            if (slot + 1) * members <= tiles:
                body()
            else:
                pl.when(slot * members + mine < tiles)(body)

        def rows_at(r, column):
            return pl.multiple_of((r * columns + column) * twice, twice)

        def over(slot, r, e):
            column = (grid.column + e) % columns
            return remote(
                g_ref.at[:, pl.ds(rows_at(r, column), twice), lanes(slot)],
                near.at[slot, e - 1, :, pl.ds(r * twice, twice)],
                push.at[slot, r, e],
                pull.at[slot, e],
                grid.where(grid.row, column, grid.core),
            )

        def spot(slot):
            return o_ref.at[:, :, pl.ds(pl.multiple_of((slot * members + mine) * LANES, LANES), LANES)]

        def piece(slot, member):
            return stage.at[slot, :, pl.ds(pl.multiple_of(member * depth, depth), depth)]

        def out(slot, e):
            member = mine ^ e
            return remote(
                piece(slot, member),
                spot(slot),
                send.at[slot, e],
                recv,
                grid.where(member // 2, grid.column, member % 2),
            )

        for slot in range(slots):

            def begin():
                for e in range(1, columns):
                    for r in range(lines):
                        over(slot, r, e).start()

            guarded(slot, begin)
        yield True
        for slot in range(slots):

            def add_up():
                for e in range(1, columns):
                    pltpu.make_async_copy(near.at[slot, e - 1], near.at[slot, e - 1], pull.at[slot, e]).wait()

                def add(i, carry):
                    for r in range(lines):
                        here = pl.ds(pl.multiple_of(rows_at(r, grid.column) + i * 16, 16), 16)
                        there = pl.ds(pl.multiple_of(r * twice + i * 16, 16), 16)
                        for kind in range(kinds):
                            value = g_ref[kind, here, lanes(slot)].astype(jnp.float32)
                            for e in range(1, columns):
                                value = value + near[slot, e - 1, kind, there].astype(jnp.float32)
                            stage[slot, kind, there] = value.astype(stage.dtype)
                    return carry

                lax.fori_loop(0, twice // 16, add, 0)
                for e in range(1, members):
                    out(slot, e).start()
                pltpu.make_async_copy(piece(slot, mine), spot(slot), recv).start()

            guarded(slot, add_up)
            yield True
        pltpu.make_async_copy(o_ref, o_ref, recv).wait()
        for slot in range(slots):

            def finish():
                for e in range(1, columns):
                    for r in range(lines):
                        over(slot, r, e).wait_send()
                for e in range(1, members):
                    out(slot, e).wait_send()

            guarded(slot, finish)

    return Task(
        [g],
        [VMEM],
        [jax.ShapeDtypeStruct((kinds, depth, width), g.dtype)],
        [VMEM],
        [
            pltpu.VMEM((slots, columns - 1, kinds, members * depth, LANES), g.dtype),
            pltpu.VMEM((slots, kinds, members * depth, LANES), g.dtype),
            dma((slots, lines, columns)),
            dma((slots, columns)),
            dma((slots, members)),
            dma,
        ],
        functools.partial(unit_targets, count),
        run,
        pace,
    )


def window(most):
    def bounds(tokens):
        first = lax.axis_index("dp") * tokens
        return jnp.maximum(first - most + 1, 0) // KEYS, (first + tokens - 1) // KEYS + 1, first

    return bounds


def attend(most, begin, q, kv, pace=1):
    tokens, heads = q.shape[0], q.shape[1] // HEAD_SIZE

    def run(begin_ref, q_ref, kv_ref, o_ref, lse_ref):
        low, high, first = window(most)(tokens)
        begin = begin_ref[...]
        index = first + lax.broadcasted_iota(jnp.int32, (tokens, 1), 0)
        lane = lax.broadcasted_iota(jnp.int32, (tokens, HEAD_SIZE), 1)
        key_lane = lax.broadcasted_iota(jnp.int32, (tokens, KEYS), 1)
        yield True
        for h in range(heads):
            cols = slice(h * HEAD_SIZE, (h + 1) * HEAD_SIZE)

            def step(block, state):
                top, mass, total = state
                start = pl.multiple_of(block * KEYS, KEYS)
                keys = kv_ref[pl.ds(start, KEYS), :HEAD_SIZE]
                values = kv_ref[pl.ds(start, KEYS), HEAD_SIZE:]
                scores = lax.dot_general(
                    q_ref[:, cols], keys, (((1,), (1,)), ((), ())), preferred_element_type=jnp.float32
                )
                at = key_lane + start
                scores = jnp.where((at >= begin) & (at <= index), scores * SCALE2, masked_score)
                best = jnp.maximum(top, jnp.max(scores, axis=1, keepdims=True))
                fade = jnp.exp2(top - best)
                probs = jnp.exp2(scores - best)
                mass = mass * fade + jnp.sum(probs, axis=1, keepdims=True)
                total = total * fade + jnp.dot(
                    probs.astype(jnp.bfloat16), values, preferred_element_type=jnp.float32
                )
                return best, mass, total

            top, mass, total = lax.fori_loop(
                low,
                high,
                step,
                (
                    jnp.full((tokens, 1), masked_score, jnp.float32),
                    jnp.zeros((tokens, 1), jnp.float32),
                    jnp.zeros((tokens, HEAD_SIZE), jnp.float32),
                ),
            )
            o_ref[:, cols] = total / mass
            lse = top + jnp.log2(mass)
            lse_ref[...] = jnp.where(lane == h, lse, 0.0 if h == 0 else lse_ref[...])
            yield True

    return Task(
        [begin, q, kv],
        [VMEM] * 3,
        [jax.ShapeDtypeStruct(q.shape, jnp.float32), jax.ShapeDtypeStruct((tokens, HEAD_SIZE), jnp.float32)],
        [VMEM] * 2,
        [],
        None,
        run,
        pace,
    )


def attend_back(most, begin, q, kv, lse, raw, do, pace=1):
    tokens, heads = q.shape[0], q.shape[1] // HEAD_SIZE
    across = (((1,), (1,)), ((), ()))
    down = (((0,), (0,)), ((), ()))

    def run(begin_ref, q_ref, kv_ref, lse_ref, raw_ref, do_ref, dq_ref, dkv_ref, delta_ref):
        low, high, first = window(most)(tokens)
        begin = begin_ref[...]
        index = first + lax.broadcasted_iota(jnp.int32, (tokens, 1), 0)
        lane = lax.broadcasted_iota(jnp.int32, (tokens, HEAD_SIZE), 1)
        key_lane = lax.broadcasted_iota(jnp.int32, (tokens, KEYS), 1)
        table = jnp.zeros((tokens, HEAD_SIZE), jnp.float32)
        for h in range(heads):
            cols = slice(h * HEAD_SIZE, (h + 1) * HEAD_SIZE)
            delta = jnp.sum(do_ref[:, cols].astype(jnp.float32) * raw_ref[:, cols], axis=1, keepdims=True)
            table = jnp.where(lane == h, delta, table)
        delta_ref[...] = table
        dq_ref[...] = jnp.zeros_like(dq_ref)
        blocks = kv_ref.shape[0] // KEYS

        def clear(block, carry):
            rows = pl.ds(pl.multiple_of(block * KEYS, KEYS), KEYS)
            dkv_ref[rows, :] = jnp.zeros((KEYS, 2 * HEAD_SIZE), dkv_ref.dtype)
            return carry

        lax.fori_loop(0, low, clear, 0)
        lax.fori_loop(high, blocks, clear, 0)

        def step(block, carry):
            start = pl.multiple_of(block * KEYS, KEYS)
            rows = pl.ds(start, KEYS)
            keys = kv_ref[rows, :HEAD_SIZE]
            values = kv_ref[rows, HEAD_SIZE:]
            at = key_lane + start
            seen = (at >= begin) & (at <= index)
            dk = jnp.zeros((KEYS, HEAD_SIZE), jnp.float32)
            dv = jnp.zeros((KEYS, HEAD_SIZE), jnp.float32)
            for h in range(heads):
                cols = slice(h * HEAD_SIZE, (h + 1) * HEAD_SIZE)
                q = q_ref[:, cols]
                do = do_ref[:, cols]
                scores = lax.dot_general(q, keys, across, preferred_element_type=jnp.float32)
                probs = jnp.where(seen, jnp.exp2(scores * SCALE2 - lse_ref[:, h : h + 1]), 0.0)
                pull = lax.dot_general(do, values, across, preferred_element_type=jnp.float32)
                ds = (probs * (pull - delta_ref[:, h : h + 1])).astype(jnp.bfloat16)
                dq_ref[:, cols] += jnp.dot(ds, keys, preferred_element_type=jnp.float32)
                dk = dk + lax.dot_general(ds, q, down, preferred_element_type=jnp.float32)
                dv = dv + lax.dot_general(
                    probs.astype(jnp.bfloat16), do, down, preferred_element_type=jnp.float32
                )
            dkv_ref[rows, :HEAD_SIZE] = (dk * SCALE).astype(dkv_ref.dtype)
            dkv_ref[rows, HEAD_SIZE:] = dv.astype(dkv_ref.dtype)
            return carry

        parts = 3
        reach = high - low
        yield True
        for i in range(parts):
            lax.fori_loop(low + reach * i // parts, low + reach * (i + 1) // parts, step, 0)
            yield True

    return Task(
        [begin, q, kv, lse, raw, do],
        [VMEM] * 6,
        [jax.ShapeDtypeStruct(q.shape, jnp.float32), jax.ShapeDtypeStruct(kv.shape, kv.dtype)],
        [VMEM] * 2,
        [pltpu.VMEM((tokens, HEAD_SIZE), jnp.float32)],
        None,
        run,
        pace,
    )


def doc_layout(row_lengths, first_token, token_count):
    doc_ends = jnp.cumsum(row_lengths)
    doc_starts = doc_ends - row_lengths
    token_index = first_token + jnp.arange(token_count, dtype=jnp.int32)
    doc_begin = jnp.max(
        jnp.where(doc_starts[None, :] <= token_index[:, None], doc_starts[None, :], 0), axis=1
    )
    return (doc_begin, token_index - doc_begin)


def rope_tables(positions):
    freq = rope_base ** (-jnp.arange(0, HEAD_SIZE, 2, dtype=jnp.float32) / HEAD_SIZE)
    angle = positions.astype(jnp.float32)[:, None] * freq[None, :]
    angle = jnp.concatenate([angle, angle], axis=1)
    return (jnp.cos(angle)[:, None, :], jnp.sin(angle)[:, None, :])


def rotary_apply(values, cosine_table, sine_table):
    half_width = values.shape[-1] // 2
    turned = jnp.concatenate([-values[..., half_width:], values[..., :half_width]], axis=-1)
    return values * cosine_table + turned * sine_table


def unrotate(grads, cosine_table, sine_table):
    half_width = grads.shape[-1] // 2
    scaled_grad = grads * sine_table
    back_part = jnp.concatenate(
        [scaled_grad[..., half_width:], -scaled_grad[..., :half_width]], axis=-1
    )
    return grads * cosine_table + back_part


def rms_scale(values):
    return lax.rsqrt(jnp.mean(values * values, axis=-1, keepdims=True) + norm_epsilon)


def norm_back(grad_out, inputs, scale, gain):
    weighted = grad_out * gain
    return scale * weighted - inputs * scale**3 * jnp.mean(
        weighted * inputs, axis=-1, keepdims=True
    )


def dot(a, b, dims=((1,), (0,))):
    return lax.dot_general(a, b, (dims, ((), ())), preferred_element_type=jnp.float32)


across_dims = ((1,), (1,))
token_dims = ((0,), (0,))


def longest(token_count):
    return 2048 if token_count == 4096 else token_count


def body(
    count,
    layer_in,
    gain_attn,
    q_weight,
    q_bias,
    key_weight,
    key_bias,
    value_weight,
    value_bias,
    o_weight,
    gain_mlp,
    gate_weight,
    up_weight,
    down_weight,
    row_lengths,
    source_ids,
    source_weights,
    out_grad,
):
    f32, bf16 = jnp.float32, jnp.bfloat16
    tok_rows, width = layer_in.shape
    part = tok_rows // 2
    half = lax.axis_index("head")
    first_token = lax.axis_index("dp") * tok_rows
    doc_begin, positions = doc_layout(row_lengths, first_token, tok_rows)
    cosine_table, sine_table = rope_tables(positions)
    q_cols = q_weight.shape[1]
    kv_cols = key_weight.shape[1]
    heads = q_cols // HEAD_SIZE
    ff_cols = gate_weight.shape[1]

    def mine(rows):
        return lax.dynamic_slice_in_dim(rows, half * part, part, 0)

    def other(rows):
        return lax.dynamic_slice_in_dim(rows, (1 - half) * part, part, 0)

    def join(own, peer):
        return jnp.where(half == 0, jnp.concatenate([own, peer]), jnp.concatenate([peer, own]))

    attn_local = jnp.concatenate([q_weight, key_weight, value_weight, o_weight.T], axis=1)
    picked = source_ids[:, None] == jnp.arange(source_weights.shape[0], dtype=jnp.int32)[None, :]
    row_scale = (
        jnp.sum(jnp.where(picked, source_weights[None, :], 0), axis=1).astype(f32) / loss_denominator
    )
    cotangent = mine(out_grad).astype(f32) * mine(row_scale[:, None])
    ((attn_full,), (grad_all,)) = fuse(
        1, "gather_inputs", gather(attn_local, count), gather(cotangent.astype(bf16), count, tower=True)
    )
    attn_full = attn_full.reshape(width, -1)
    grad_all = grad_all.reshape(-1, width)
    qkv_cols = q_cols + 2 * kv_cols
    full_qkv = attn_full[:, :qkv_cols]
    full_o = attn_full[:, qkv_cols:]
    inputs = layer_in.astype(f32)
    scale_one = rms_scale(inputs)
    gain_one = gain_attn.astype(f32)
    normed = (inputs * scale_one * gain_one).astype(bf16)
    bias = jnp.concatenate([q_bias, key_bias, value_bias]).astype(f32)
    pre = dot(normed, full_qkv) + bias
    turned = rotary_apply(
        pre[:, : q_cols + kv_cols].reshape(tok_rows, heads + 1, HEAD_SIZE), cosine_table, sine_table
    ).reshape(tok_rows, q_cols + kv_cols)
    query_rows = turned[:, :q_cols].astype(bf16)
    kv_rows = jnp.concatenate([turned[:, q_cols:], pre[:, q_cols + kv_cols :]], axis=1).astype(bf16)
    ((kv_all,),) = fuse(2, "gather_keys", gather(kv_rows, count))
    kv_all = kv_all.reshape(-1, 2 * kv_cols)
    begin = doc_begin[:, None].astype(jnp.int32)
    most = longest(count * tok_rows)
    mlp_local = jnp.stack([gate_weight, up_weight, down_weight.T])
    ((attended_raw, row_lse), (mlp_full,)) = fuse(
        3, "attend_spread", attend(most, begin, query_rows, kv_all), spread(mlp_local, count)
    )
    attended = attended_raw.astype(bf16)
    branch_part = dot(attended, full_o, across_dims)
    ((branch_peer,),) = fuse(4, "swap_branch", swap([other(branch_part).astype(bf16)]))
    hidden = mine(inputs) + (mine(branch_part) + branch_peer.astype(f32))
    scale_two = rms_scale(hidden)
    gain_two = gain_mlp.astype(f32)
    normed_mlp = (hidden * scale_two * gain_two).astype(bf16)
    ((rows_all,),) = fuse(5, "gather_rows", gather(normed_mlp, count, tower=True))
    rows_all = rows_all.reshape(-1, width)

    full_gate, full_up, full_down = mlp_full[0], mlp_full[1], mlp_full[2]
    gate_act = dot(rows_all, full_gate)
    up_act = dot(rows_all, full_up)
    sigmoid_gate = jax.nn.sigmoid(gate_act)
    silu_gate = gate_act * sigmoid_gate
    active = (silu_gate * up_act).astype(bf16)
    d_active = dot(grad_all, full_down)
    d_gate = (d_active * up_act * sigmoid_gate * (1.0 + gate_act * (1.0 - sigmoid_gate))).astype(bf16)
    d_up = (d_active * silu_gate).astype(bf16)
    mlp_part = dot(active, full_down, across_dims).astype(bf16)
    norm_two_part = (dot(d_gate, full_gate, across_dims) + dot(d_up, full_up, across_dims)).astype(bf16)
    mlp_grads = jnp.stack(
        [
            dot(rows_all, d_gate, token_dims).astype(bf16),
            dot(rows_all, d_up, token_dims).astype(bf16),
            dot(grad_all, active, token_dims).astype(bf16),
        ]
    )
    d_normed_mlp = scatter_all(norm_two_part, count, 8, "scatter_rows", tower=True)
    gain_two_local = jnp.sum(d_normed_mlp * hidden * scale_two, axis=0)
    d_hidden = cotangent + norm_back(d_normed_mlp, hidden, scale_two, gain_two)
    branch_own = d_hidden.astype(bf16)
    ((branch_peer,),) = fuse(16, "swap_grad", swap([branch_own]))
    branch_grad = join(branch_own, branch_peer)
    out_proj_grad = dot(branch_grad, attended, token_dims)
    d_attended = dot(branch_grad, full_o).astype(bf16)
    ((d_query, d_kv), (mlp_part_sums,)) = fuse(
        17,
        "attend_back_collect",
        attend_back(most, begin, query_rows, kv_all, row_lse, attended_raw, d_attended),
        collect(mlp_grads, count, ff_cols),
    )
    mlp_part_sums = mlp_part_sums.astype(f32)
    kv_sums = scatter_all(d_kv, count, 18, "scatter_keys")
    d_queries = (d_query * SCALE).astype(bf16).astype(f32)
    d_key_rot = kv_sums[:, :kv_cols].astype(bf16).astype(f32)
    d_value_rows = kv_sums[:, kv_cols:].astype(bf16)
    d_turned = jnp.concatenate([d_queries, d_key_rot], axis=1).reshape(tok_rows, heads + 1, HEAD_SIZE)
    d_pre = jnp.concatenate(
        [
            unrotate(d_turned, cosine_table, sine_table).reshape(tok_rows, q_cols + kv_cols).astype(bf16),
            d_value_rows,
        ],
        axis=1,
    )
    bias_local = jnp.sum(d_pre.astype(f32), axis=0)
    qkv_grad = dot(normed, d_pre, token_dims)
    attn_grads = jnp.concatenate([qkv_grad, out_proj_grad], axis=1).astype(bf16)
    norm_one_part = dot(d_pre, full_qkv, across_dims)
    norm_send = other(norm_one_part).astype(bf16)
    if count <= 16:
        ((attn_part,), (mlp_out,), (norm_peer,)) = fuse(
            21, "scatter_last", scatter(attn_grads, count), scatter(mlp_part, count, tower=True), swap([norm_send])
        )
    else:
        attn_part = scatter_all(attn_grads, count, 21, "scatter_attn")
        mlp_out = scatter_all(mlp_part, count, 25, "scatter_out", tower=True)
        ((norm_peer,),) = fuse(33, "swap_norm", swap([norm_send]))
    layer_out_own = (hidden + mlp_out).astype(bf16)
    d_normed = mine(norm_one_part) + norm_peer.astype(f32)
    inputs_own = mine(inputs)
    scale_own = mine(scale_one)
    gain_one_local = jnp.sum(d_normed * inputs_own * scale_own, axis=0)
    layer_in_grad_own = (d_hidden + norm_back(d_normed, inputs_own, scale_own, gain_one)).astype(bf16)

    small = jnp.concatenate([bias_local, gain_one_local, gain_two_local]).reshape(-1, LANES)
    ((small_all,), (layer_in_grad_peer, layer_out_peer)) = fuse(
        34, "gather_sums", gather(small, count, both=True), swap([layer_in_grad_own, layer_out_own])
    )
    small_all = small_all.reshape(count, 2, -1)
    small_sum = jnp.sum(small_all[:, 0], axis=0)
    gains = (small_sum[qkv_cols:] + jnp.sum(small_all[:, 1, qkv_cols:], axis=0)).reshape(2, width)
    layer_in_grad = join(layer_in_grad_own, layer_in_grad_peer)
    layer_out = join(layer_out_own, layer_out_peer)
    return (
        layer_out,
        layer_in_grad,
        gains[0],
        attn_part[:, :q_cols],
        small_sum[:q_cols],
        attn_part[:, q_cols : q_cols + kv_cols],
        small_sum[q_cols : q_cols + kv_cols],
        attn_part[:, q_cols + kv_cols : qkv_cols],
        small_sum[q_cols + kv_cols : qkv_cols],
        attn_part[:, qkv_cols:].T,
        gains[1],
        mlp_part_sums[0],
        mlp_part_sums[1],
        mlp_part_sums[2].T,
    )


def solution(mesh):
    placed = (
        P("dp", None),
        P(),
        P("dp", "head"),
        P("head"),
        P("dp", "head"),
        P("head"),
        P("dp", "head"),
        P("head"),
        P("head", "dp"),
        P(),
        P("dp", "head"),
        P("dp", "head"),
        P("head", "dp"),
        P(),
        P("dp"),
        P(),
        P("dp", None),
    )
    return jax.shard_map(
        functools.partial(body, mesh.shape["dp"]),
        mesh=mesh,
        in_specs=placed,
        out_specs=(
            P("dp", None),
            P("dp", None),
            P(),
            P("dp", "head"),
            P("head"),
            P("dp", "head"),
            P("head"),
            P("dp", "head"),
            P("head"),
            P("head", "dp"),
            P(),
            P("dp", "head"),
            P("dp", "head"),
            P("head", "dp"),
        ),
        check_vma=False,
    )
```

time: 1990 us -> 695 us (0.35)
  waiting for transfers between devices: 1660 us -> 0 us
  Pallas kernels: 0 us -> 538 us
  blocking collectives: 98 us -> 0 us
  matrix products: 151 us -> 82.3 us
    reduce_scatter x9 -> x0, waiting for transfers between devices: 1170 us -> none  [the longest x1 270 us: body(): lax.psum_scatter(mlp_parts[0], 'dp', scatter_dimension=0, tiled=True)]
    pallas_call x0 -> x11, Pallas kernels: none -> 538 us  [fuse(): pl.pallas_call(kernel, out_shape=[o for t in tasks for o in t.outs], in_s...]
    all_gather x7 -> x0, waiting for transfers between devices: 425 us -> none  [the longest x1 108 us: body(): lax.all_gather(gate_weight, 'dp', axis=0, tiled=True)]
    dot_general x28 -> x15, matrix products: 151 us -> 82.3 us  [dot(): lax.dot_general(a, b, (dims, ((), ())), preferred_element_type=jnp.float32)]
    psum x3 -> x0, waiting for transfers between devices: 62.1 us -> none  [the longest x1 32.1 us: body(): lax.psum(norm_two_part.astype(jnp.bfloat16), 'head').astype(jnp.float32)]
    psum x1 -> x0, blocking collectives: 55 us -> none  [body(): lax.psum((query_bias_local, key_bias_local, value_bias_local, gain_one_lo...]
    all_gather x2 -> x0, blocking collectives: 43 us -> none  [the longest x1 24.3 us: body(): lax.all_gather(key_weight, 'dp', axis=0, tiled=True)]
  transfers between devices with their start and end apart: 19 -> 0, of which waited for: 17 -> 0; matrix products, arithmetic and copies ran while one was open for 6% -> 0% of each run, Pallas kernels for 0% -> 0%
where the time goes in v1:
time: 695 us; the launch traced here: 687 us
  Pallas kernels  538 us (77%)
  matrix products  82.3 us (12%)
  other arithmetic  39.7 us (6%)
  local copies, waits for them, and re-layouts  24.3 us (3%)
    pallas_call x11, Pallas kernels, fuse(): pl.pallas_call(kernel, out_shape=[o for t in tasks for o in t.outs], in_s...  538 us
    dot_general x15, matrix products, dot(): lax.dot_general(a, b, (dims, ((), ())), preferred_element_type=jnp.float32)  82.3 us

profile of v1, /device:TPU:1, one launch (start us, length us, event | category | flops | bytes accessed | tf_op | source)
XLA Modules:
  0.0 686.5 jit_solution(7341677617642500996)
XLA Ops:
  0.7 0.8 select_reduce_fusion
  2.1 1.9 fusion.35.refs_1_
  4.0 1.8 maximum_bitcast_fusion.refs_0_
  5.8 67.4 %gather_inputs.1 = (bf16[16,1,96,1792]{3,2,1,0:T(8,128)(2,1)}, bf16[16,1,128,1536]{3,2,1,0:T(8,128)(2,1)}) custom-call(bf16[1,96,1792]{2,1,0:T(8,128)(2,1)} %maximum_bitcast_fusion.refs_0_, bf16[1,128,1536]{2,1,0:T(8,128)(2,1)} %fusion.35.refs_1_), custom_call_target="tpu_custom_call" | custom-call | tf_op jit(solution)/shard_map/gather_inputs/pallas_call | solution.py:122
  73.2 0.7 convert_element_type.117
  74.2 2.9 fusion.28
  77.2 1.0 copy-done.6
  79.1 1.1 fusion.40
  80.9 1.0 mul.253
  82.2 1.3 add_convert_fusion.2
  83.5 1.1 fusion.41
  85.3 24.3 %gather_keys.1 = bf16[16,1,256,256]{3,2,1,0:T(8,128)(2,1)} custom-call(bf16[1,256,256]{2,1,0:T(8,128)(2,1)} %pad_maximum_fusion.8.refs_0_), custom_call_target="tpu_custom_call" | custom-call | tf_op jit(solution)/shard_map/gather_keys/pallas_call | solution.py:122
  109.6 0.8 slice.131.refs_1_
  110.4 0.8 copy.42.refs_0_
  111.2 3.0 pad_maximum_fusion.2.refs_3_
  114.1 95.3 %attend_spread.1 = (f32[256,768]{1,0:T(8,128)}, f32[256,128]{1,0:T(8,128)}, bf16[3,1536,640]{2,1,0:T(8,128)(2,1)}) custom-call(s32[256,1]{1,0:T(8,128)} %copy.42.refs_0_, bf16[256,768]{1,0:T(8,128)(2,1)} %slice.131.refs_1_, bf16[4096,256]{1,0:T(8,128)(2,1)} %bitcast.87, bf16[3,96,4480]{2,1,0:T(8,128)(2,1)} %pad_maximum_fusion.2.refs_3_), custom_call_target="tpu_custom_call" | custom-call | tf_op jit(solution)/shard_map/attend_spread/pallas_call | solution.py:122
  209.4 9.3 %fusion.20 = f32[2048,640]{1,0:T(8,128)} fusion(bf16[2048,1536]{1,0:T(8,128)(2,1)} %bitcast.112, bf16[3,1536,640]{2,1,0:T(8,128)(2,1)} %get-tuple-element.32), kind=kOutput, calls=%fused_computation.34 | convolution fusion | flops 4026531840 | bytes 13500416 | tf_op jit(solution)/shard_map/dot_general | solution.py:844
  218.7 2.5 fusion.10
  221.2 0.9 dynamic-slice_convert_fusion.1.refs_0_
  222.5 12.1 %swap_branch.1 = bf16[128,1536]{1,0:T(8,128)(2,1)} custom-call(bf16[128,1536]{1,0:T(8,128)(2,1)} %dynamic-slice_convert_fusion.1.refs_0_), custom_call_target="tpu_custom_call" | custom-call | tf_op jit(solution)/shard_map/swap_branch/pallas_call | solution.py:122
  234.8 1.2 copy-done.2
  236.2 0.9 fusion.36.refs_0_
  237.1 40.9 %gather_rows.1 = bf16[16,1,128,1536]{3,2,1,0:T(8,128)(2,1)} custom-call(bf16[1,128,1536]{2,1,0:T(8,128)(2,1)} %fusion.36.refs_0_), custom_call_target="tpu_custom_call" | custom-call | tf_op jit(solution)/shard_map/gather_rows/pallas_call | solution.py:122
  278.0 7.9 %fusion.14 = f32[2048,640]{1,0:T(8,128)S(1)} fusion(bf16[2048,1536]{1,0:T(8,128)(2,1)} %bitcast.89, bf16[3,1536,640]{2,1,0:T(8,128)(2,1)} %get-tuple-element.32), kind=kOutput, calls=%fused_computation.28 | convolution fusion | flops 4026531840 | bytes 13500416 | tf_op jit(solution)/shard_map/dot_general | solution.py:844
  285.9 11.0 %multiply_convert_fusion = (bf16[2048,640]{1,0:T(8,128)(2,1)}, bf16[2048,640]{1,0:T(8,128)(2,1)S(1)}, bf16[2048,640]{1,0:T(8,128)(2,1)}) fusion(f32[2048,640]{1,0:T(8,128)S(1)} %fusion.14, f32[2048,640]{1,0:T(8,128)} %fusion.20, bf16[2048,1536]{1,0:T(8,128)(2,1)S(1)} %bitcast.90, bf16[3,1536,640]{2,1,0:T(8,128)(2,1)} %get-tuple-element.32), kind=kOutput, calls=%fused_computation.4 | convolution fusion | flops 4046192640 | bytes 26607616 | tf_op jit(solution)/shard_map/dot_general | solution.py:844
  296.9 1.5 copy-done.34
  298.4 5.4 fusion.1
  303.8 5.4 fusion.2
  309.2 5.5 fusion.3
  314.7 3.1 pad_maximum_fusion.refs_6_
  317.9 6.8 fusion.12
  324.7 8.6 %add_convert_fusion = bf16[2048,1536]{1,0:T(8,128)(2,1)} fusion(f32[2048,1536]{1,0:T(8,128)S(1)} %fusion.12, bf16[2048,640]{1,0:T(8,128)(2,1)S(1)} %copy-done.37, bf16[3,1536,640]{2,1,0:T(8,128)(2,1)} %get-tuple-element.32), kind=kOutput, calls=%fused_computation | convolution fusion | flops 4032823296 | bytes 23461888 | tf_op jit(solution)/shard_map/dot_general | solution.py:844
  333.3 56.6 %scatter_rows0.1 = f32[128,1536]{1,0:T(8,128)} custom-call(bf16[16,128,1536]{2,1,0:T(8,128)(2,1)} %bitcast.94), custom_call_target="tpu_custom_call" | custom-call | tf_op jit(solution)/shard_map/scatter_rows0/pallas_call | solution.py:122
  389.9 1.3 multiply_reduce_fusion.4
  391.3 2.6 fusion.47
  393.8 11.6 %swap_grad.1 = bf16[128,1536]{1,0:T(8,128)(2,1)} custom-call(bf16[128,1536]{1,0:T(8,128)(2,1)} %get-tuple-element.48.refs_0_), custom_call_target="tpu_custom_call" | custom-call | tf_op jit(solution)/shard_map/swap_grad/pallas_call | solution.py:122
  405.4 3.7 fusion.31.refs_5_
  409.1 84.3 %attend_back_collect.1 = (f32[256,768]{1,0:T(8,128)}, bf16[4096,256]{1,0:T(8,128)(2,1)}, bf16[3,96,4480]{2,1,0:T(8,128)(2,1)}) custom-call(s32[256,1]{1,0:T(8,128)} %copy.42.refs_0_, bf16[256,768]{1,0:T(8,128)(2,1)} %slice.131.refs_1_, bf16[4096,256]{1,0:T(8,128)(2,1)} %bitcast.88, f32[256,128]{1,0:T(8,128)} %get-tuple-element.30.refs_3_, ...), custom_call_target="tpu_custom_call" | custom-call | tf_op jit(solution)/shard_map/attend_back_collect/pallas_call | solution.py:122
  493.4 26.1 %scatter_keys0.1 = f32[256,256]{1,0:T(8,128)} custom-call(bf16[16,256,256]{2,1,0:T(8,128)(2,1)} %bitcast.102), custom_call_target="tpu_custom_call" | custom-call | tf_op jit(solution)/shard_map/scatter_keys0/pallas_call | solution.py:122
  519.5 1.0 convert.26
  520.5 1.2 multiply_convert_fusion.4
  521.7 0.7 copy-done.5
  522.5 1.0 maximum_convert_fusion
  523.5 2.4 copy.45
  525.9 1.3 broadcast_multiply_fusion
  527.2 1.0 pad_maximum_fusion.3
  528.2 2.4 copy.46
  530.6 1.4 add_convert_fusion.1
  532.1 3.0 fusion.4
  535.0 0.9 dynamic-slice_convert_fusion.refs_2_
  536.0 1.1 convolution_convert_fusion.1
  537.3 0.8 convolution_convert_fusion.2
  538.1 2.9 pad_maximum_fusion.1.refs_0_
  541.1 8.5 %convolution_convert_fusion = bf16[2048,1536]{1,0:T(8,128)(2,1)} fusion(bf16[2048,640]{1,0:T(8,128)(2,1)S(1)} %copy-done.39, bf16[3,1536,640]{2,1,0:T(8,128)(2,1)} %get-tuple-element.32), kind=kOutput, calls=%fused_computation.1 | convolution fusion | flops 4029677568 | bytes 10878976 | tf_op jit(solution)/shard_map/dot_general | solution.py:844
  549.6 70.5 %scatter_last.1 = (f32[96,1792]{1,0:T(8,128)}, f32[128,1536]{1,0:T(8,128)}, bf16[128,1536]{1,0:T(8,128)(2,1)}) custom-call(bf16[16,96,1792]{2,1,0:T(8,128)(2,1)} %pad_maximum_fusion.1.refs_0_, bf16[16,128,1536]{2,1,0:T(8,128)(2,1)} %bitcast.93, bf16[128,1536]{1,0:T(8,128)(2,1)} %dynamic-slice_convert_fusion.refs_2_), custom_call_target="tpu_custom_call" | custom-call | tf_op jit(solution)/shard_map/scatter_last/pallas_call | solution.py:122
  620.1 2.1 add_convert_fusion.4.refs_2_
  622.3 1.5 multiply_reduce_fusion.1
  623.8 1.1 add_convert_fusion.3.refs_1_
  625.6 49.4 %gather_sums.1 = (f32[16,2,32,128]{3,2,1,0:T(8,128)}, bf16[128,1536]{1,0:T(8,128)(2,1)}, bf16[128,1536]{1,0:T(8,128)(2,1)}) custom-call(f32[1,32,128]{2,1,0:T(8,128)} %maximum_bitcast_fusion.1.refs_0_, bf16[128,1536]{1,0:T(8,128)(2,1)} %add_convert_fusion.3.refs_1_, bf16[128,1536]{1,0:T(8,128)(2,1)} %add_convert_fusion.4.refs_2_), custom_call_target="tpu_custom_call" | custom-call | tf_op jit(solution)/shard_map/gather_sums/pallas_call | solution.py:122
  675.0 1.4 reshape.298
  677.4 2.2 maximum_select_fusion.2
  679.7 1.0 maximum_select_fusion.1
  681.8 0.8 slice_bitcast_fusion.3
  683.6 2.4 slice_bitcast_fusion
  (119 shorter events, 8.6 us)
Async XLA Ops:
  0.6 73.3 %copy-start.9 = (bf16[256,1536]{1,0:T(8,128)(2,1)S(1)}, bf16[256,1536]{1,0:T(8,128)(2,1)}, u32[]{:S(2)}) copy-start(bf16[256,1536]{1,0:T(8,128)(2,1)} %param.17) | copy-start | bytes 2359300
  0.7 73.5 %copy-start.30 = (bf16[768]{0:T(1024)(128)(2,1)S(1)}, bf16[768]{0:T(1024)(128)(2,1)}, u32[]{:S(2)}) copy-start(bf16[768]{0:T(1024)(128)(2,1)} %param.20) | copy-start | bytes 4612
  0.7 73.5 %copy-start.32 = (bf16[128]{0:T(256)(128)(2,1)S(1)}, bf16[128]{0:T(256)(128)(2,1)}, u32[]{:S(2)}) copy-start(bf16[128]{0:T(256)(128)(2,1)} %param.22) | copy-start | bytes 772
  0.7 73.5 %copy-start.31 = (bf16[128]{0:T(256)(128)(2,1)S(1)}, bf16[128]{0:T(256)(128)(2,1)}, u32[]{:S(2)}) copy-start(bf16[128]{0:T(256)(128)(2,1)} %param.24) | copy-start | bytes 772
  1.6 0.5 copy-start.28
  74.2 3.0 copy-start.26
  77.1 1.0 copy-start.6
  78.1 0.7 copy-start.33
  80.3 0.7 copy-start.18
  83.5 27.6 %copy-start.20 = (bf16[4480,96]{0,1:T(8,128)(2,1)S(1)}, bf16[4480,96]{0,1:T(8,128)(2,1)}, u32[]{:S(2)}) copy-start(bf16[4480,96]{0,1:T(8,128)(2,1)} %param.29) | copy-start | bytes 2580484
  83.5 27.6 %copy-start.21 = (bf16[96,4480]{1,0:T(8,128)(2,1)S(1)}, bf16[96,4480]{1,0:T(8,128)(2,1)}, u32[]{:S(2)}) copy-start(bf16[96,4480]{1,0:T(8,128)(2,1)} %param.28) | copy-start | bytes 2580484
  209.4 9.3 %copy-start.7 = (f32[256,768]{1,0:T(8,128)S(1)}, f32[256,768]{1,0:T(8,128)}, u32[]{:S(2)}) copy-start(f32[256,768]{1,0:T(8,128)} %get-tuple-element.29.refs_4_) | copy-start | bytes 2359300
  221.2 1.3 copy-start.1
  234.5 1.4 copy-start.2
  234.5 1.5 copy-start.16
  234.6 1.7 copy-start.25
  278.0 7.9 %copy-start = (bf16[16,1,128,1536]{3,2,1,0:T(8,128)(2,1)S(1)}, bf16[16,1,128,1536]{3,2,1,0:T(8,128)(2,1)}, u32[]{:S(2)}) copy-start(bf16[16,1,128,1536]{3,2,1,0:T(8,128)(2,1)} %gather_rows.1) | copy-start | bytes 18874372
  296.9 1.5 copy-start.34
  298.4 5.4 copy-start.36
  298.4 10.8 %slice-start = ((s8[6291456]{0:T(1024)(128)(4,1)}), s8[4194304]{0:T(1024)(128)(4,1)S(1)}, s32[]{:S(2)}) async-start(s8[6291456]{0:T(1024)(128)(4,1)} %bitcast.113), calls=%async_computation | async-start | bytes 8388608
  303.8 5.4 slice-start.1
  303.8 5.4 copy-start.38
  314.7 3.1 copy-start.35
  317.9 6.8 copy-start.37
  333.3 58.0 %copy-start.29 = (f32[128]{0:T(128)S(1)}, f32[128]{0:T(128)}, u32[]{:S(2)}) copy-start(f32[128]{0:T(128)} %copy-done.28) | copy-start | bytes 1540
  519.5 6.4 copy-start.19
  521.7 0.7 copy-start.5
  532.0 3.9 copy-start.10
  532.0 3.9 copy-start.27
  535.0 2.0 copy-start.13
  535.9 1.1 copy-start.8
  535.9 1.2 copy-start.15
  535.9 1.3 copy-start.23
  538.1 3.0 copy-start.39
  620.1 3.7 copy-start.11
  620.1 3.7 copy-start.14
  620.1 3.7 copy-start.17
  624.9 52.5 %copy-start.4 = (bf16[128,1536]{1,0:T(8,128)(2,1)S(1)}, bf16[128,1536]{1,0:T(8,128)(2,1)}, u32[]{:S(2)}) copy-start(bf16[128,1536]{1,0:T(8,128)(2,1)} %add_convert_fusion.3.refs_1_) | copy-start | bytes 1179652
  624.9 54.7 %copy-start.3 = (bf16[128,1536]{1,0:T(8,128)(2,1)S(1)}, bf16[128,1536]{1,0:T(8,128)(2,1)}, u32[]{:S(2)}) copy-start(bf16[128,1536]{1,0:T(8,128)(2,1)} %add_convert_fusion.4.refs_2_) | copy-start | bytes 1179652
  625.6 56.2 %copy-start.22 = (f32[96,1792]{1,0:T(8,128)S(1)}, f32[96,1792]{1,0:T(8,128)}, u32[]{:S(2)}) copy-start(f32[96,1792]{1,0:T(8,128)} %get-tuple-element.40) | copy-start | bytes 2064388
  675.0 4.6 copy-start.24
  676.4 6.9 %copy-start.12 = (bf16[3,96,4480]{2,1,0:T(8,128)(2,1)S(1)}, bf16[3,96,4480]{2,1,0:T(8,128)(2,1)}, u32[]{:S(2)}) copy-start(bf16[3,96,4480]{2,1,0:T(8,128)(2,1)} %get-tuple-element.41) | copy-start | bytes 7741444

commit v2 on v1

--- a/solution.py
+++ b/solution.py
@@ -34,6 +34,12 @@
     )
 
 
+def reshape(x, shape):
+    if isinstance(x, jax.ShapeDtypeStruct):
+        return jax.ShapeDtypeStruct(shape, x.dtype)
+    return x.reshape(shape)
+
+
 class Grid:
     def __init__(self, count, tower=False):
         self.lines, self.columns = grid_of(count)
@@ -64,10 +70,9 @@
     scratch: list
     targets: Callable
     run: Callable
-    pace: int = 1
-
-
-def fuse(ident, name, *tasks):
+
+
+def fuse(ident, name, *tasks, order=()):
     remote_ops = any(t.targets is not None for t in tasks)
 
     def split(refs, sizes):
@@ -102,19 +107,17 @@
 
                         total = total + ok.astype(jnp.int32)
             pl.semaphore_wait(barrier, total)
-        live = [
-            (t.run(*a, *b, *c), t.pace)
+        steps = [
+            t.run(*a, *b, *c)
             for t, a, b, c in zip(tasks, split(ins, n_in), split(outs, n_out), split(scratch, n_scratch))
         ]
+        live = set(range(len(steps)))
+        turns = list(order)
         while live:
-            kept = []
-            for steps, pace in live:
-                for _ in range(pace):
-                    if next(steps, None) is None:
-                        break
-                else:
-                    kept.append((steps, pace))
-            live = kept
+            for i in turns:
+                if i in live and next(steps[i], None) is None:
+                    live.remove(i)
+            turns = sorted(live)
 
     params = dict(vmem_limit_bytes=60 << 20)
     if remote_ops:
@@ -131,13 +134,13 @@
     return split(flat, n_out)
 
 
-def gather(x, count, tower=False, pieces=1, both=False, pace=1):
+def gather(x, count, tower=False, pieces=1, both=False):
     lines, columns = grid_of(count)
     across = 2 if tower else columns
     members = lines * across * 2
     shape = x.shape
     pieces = 1 if both else pieces
-    x = x.reshape((pieces, shape[0] // pieces) + shape[1:])
+    x = reshape(x, (pieces, shape[0] // pieces) + shape[1:])
     copies = 2 if both else pieces
 
     def hops_of(grid):
@@ -240,18 +243,17 @@
         [dma((5, members, copies)), dma((members, copies)), dma, dma((2,))],
         targets,
         run,
-        pace,
-    )
-
-
-def scatter(x, count, tower=False, dtype=jnp.float32, pace=1):
+    )
+
+
+def scatter(x, count, tower=False, dtype=jnp.float32):
     lines, columns = grid_of(count)
     across = 2 if tower else columns
     members = lines * across * 2
     block = (x.shape[0] // members,) + x.shape[1:]
     height = block[0]
     step = 16
-    x = x.reshape((members,) + block)
+    x = reshape(x, (members,) + block)
 
     def targets():
         grid = Grid(count, tower)
@@ -367,7 +369,6 @@
         ],
         targets,
         run,
-        pace,
     )
 
 
@@ -380,7 +381,7 @@
     return parts[0] if cuts == 1 else jnp.concatenate(parts, axis=1)
 
 
-def swap(arrays, pace=1):
+def swap(arrays):
     parts = len(arrays)
 
     def targets():
@@ -405,7 +406,6 @@
         [dma((parts,)), dma((parts,))],
         targets,
         run,
-        pace,
     )
 
 
@@ -422,7 +422,7 @@
     return found
 
 
-def spread(w, count, pace=1):
+def spread(w, count):
     lines, columns = grid_of(count)
     kinds, depth, width = w.shape
     tiles = width // LANES
@@ -538,11 +538,10 @@
         ],
         functools.partial(unit_targets, count),
         run,
-        pace,
-    )
-
-
-def collect(g, count, width, pace=1):
+    )
+
+
+def collect(g, count, width):
     lines, columns = grid_of(count)
     kinds, rows, span = g.shape
     tiles = width // LANES
@@ -653,7 +652,6 @@
         ],
         functools.partial(unit_targets, count),
         run,
-        pace,
     )
 
 
@@ -665,7 +663,7 @@
     return bounds
 
 
-def attend(most, begin, q, kv, pace=1):
+def attend(most, begin, q, kv):
     tokens, heads = q.shape[0], q.shape[1] // HEAD_SIZE
 
     def run(begin_ref, q_ref, kv_ref, o_ref, lse_ref):
@@ -720,11 +718,76 @@
         [],
         None,
         run,
-        pace,
-    )
-
-
-def attend_back(most, begin, q, kv, lse, raw, do, pace=1):
+    )
+
+
+def forward(most, count, begin, q, kv, attn, x, gain):
+    tokens, width = q.shape[0], x.shape[1]
+    part, inner = x.shape[0], q.shape[1]
+    core = attend(most, begin, q, kv)
+    rows = gather(jax.ShapeDtypeStruct((part, width), jnp.bfloat16), count, tower=True)
+    pair = swap([jax.ShapeDtypeStruct((part, width), jnp.bfloat16)])
+    n_rows, n_pair = len(rows.scratch), len(pair.scratch)
+    columns = 256
+    skip = attn.shape[1] - inner
+
+    def run(begin_ref, q_ref, kv_ref, attn_ref, x_ref, gain_ref, o_ref, lse_ref, hidden_ref, rows_ref, *scratch):
+        sent, got, normed, whole = scratch[:4]
+        half = lax.axis_index("head")
+        yield from core.run(begin_ref, q_ref, kv_ref, o_ref, lse_ref)
+
+        def project(i, carry):
+            cols = pl.ds(pl.multiple_of(i * columns, columns), columns)
+            whole[:, cols] = lax.dot_general(
+                o_ref[...].astype(jnp.bfloat16),
+                attn_ref[cols, skip:],
+                (((1,), (1,)), ((), ())),
+                preferred_element_type=jnp.float32,
+            )
+            return carry
+
+        lax.fori_loop(0, width // columns, project, 0)
+
+        def of(h):
+            return pl.ds(pl.multiple_of(h * part, part), part)
+
+        sent[...] = whole[of(1 - half)].astype(jnp.bfloat16)
+        yield from pair.run(sent, got, *scratch[4 : 4 + n_pair])
+        step = 16
+
+        def norm(i, carry):
+            here = pl.ds(pl.multiple_of(i * step, step), step)
+            there = pl.ds(pl.multiple_of(half * part + i * step, step), step)
+            hidden = x_ref[here].astype(jnp.float32) + (whole[there] + got[here].astype(jnp.float32))
+            hidden_ref[here] = hidden
+            normed[0, here] = (hidden * rms_scale(hidden) * gain_ref[...]).astype(jnp.bfloat16)
+            return carry
+
+        lax.fori_loop(0, part // step, norm, 0)
+        yield from rows.run(normed, rows_ref, *scratch[4 + n_pair :])
+
+    def targets():
+        return pair.targets() + rows.targets()
+
+    return Task(
+        [begin, q, kv, attn, x, gain],
+        [VMEM] * 6,
+        core.outs + [jax.ShapeDtypeStruct((part, width), jnp.float32)] + rows.outs,
+        [VMEM] * 3 + rows.out_specs,
+        [
+            pltpu.VMEM((part, width), jnp.bfloat16),
+            pltpu.VMEM((part, width), jnp.bfloat16),
+            pltpu.VMEM((1, part, width), jnp.bfloat16),
+            pltpu.VMEM((tokens, width), jnp.float32),
+        ]
+        + pair.scratch
+        + rows.scratch,
+        targets,
+        run,
+    )
+
+
+def attend_back(most, begin, q, kv, lse, raw, do):
     tokens, heads = q.shape[0], q.shape[1] // HEAD_SIZE
     across = (((1,), (1,)), ((), ()))
     down = (((0,), (0,)), ((), ()))
@@ -745,8 +808,7 @@
         blocks = kv_ref.shape[0] // KEYS
 
         def clear(block, carry):
-            rows = pl.ds(pl.multiple_of(block * KEYS, KEYS), KEYS)
-            dkv_ref[rows, :] = jnp.zeros((KEYS, 2 * HEAD_SIZE), dkv_ref.dtype)
+            dkv_ref[block] = jnp.zeros((KEYS, 2 * HEAD_SIZE), dkv_ref.dtype)
             return carry
 
         lax.fori_loop(0, low, clear, 0)
@@ -774,8 +836,8 @@
                 dv = dv + lax.dot_general(
                     probs.astype(jnp.bfloat16), do, down, preferred_element_type=jnp.float32
                 )
-            dkv_ref[rows, :HEAD_SIZE] = (dk * SCALE).astype(dkv_ref.dtype)
-            dkv_ref[rows, HEAD_SIZE:] = dv.astype(dkv_ref.dtype)
+            dkv_ref[block, :, :HEAD_SIZE] = (dk * SCALE).astype(dkv_ref.dtype)
+            dkv_ref[block, :, HEAD_SIZE:] = dv.astype(dkv_ref.dtype)
             return carry
 
         parts = 3
@@ -788,12 +850,14 @@
     return Task(
         [begin, q, kv, lse, raw, do],
         [VMEM] * 6,
-        [jax.ShapeDtypeStruct(q.shape, jnp.float32), jax.ShapeDtypeStruct(kv.shape, kv.dtype)],
+        [
+            jax.ShapeDtypeStruct(q.shape, jnp.float32),
+            jax.ShapeDtypeStruct((kv.shape[0] // KEYS, KEYS, kv.shape[1]), kv.dtype),
+        ],
         [VMEM] * 2,
         [pltpu.VMEM((tokens, HEAD_SIZE), jnp.float32)],
         None,
         run,
-        pace,
     )
 
 
@@ -846,6 +910,105 @@
 
 across_dims = ((1,), (1,))
 token_dims = ((0,), (0,))
+
+
+def backward(most, count, begin, q, kv, lse, raw, own, attn):
+    tokens, width = q.shape[0], own.shape[1]
+    part, inner = own.shape[0], q.shape[1]
+    core = attend_back(most, begin, q, kv, lse, raw, jax.ShapeDtypeStruct(q.shape, jnp.bfloat16))
+    d_query, d_kv = core.outs
+    sums = scatter(jax.ShapeDtypeStruct((kv.shape[0], kv.shape[1]), kv.dtype), count)
+    columns = 256
+    skip = attn.shape[1] - inner
+
+    def run(
+        begin_ref, q_ref, kv_ref, lse_ref, raw_ref, own_ref, attn_ref, dq_ref, sums_ref, branch_ref, delta, do, dkv, send, recv, *scratch
+    ):
+        half = lax.axis_index("head")
+        here = pl.ds(pl.multiple_of(half * part, part), part)
+        copy = remote(
+            own_ref, branch_ref.at[here], send, recv, {"dp": lax.axis_index("dp"), "head": 1 - half}
+        )
+        copy.start()
+        branch_ref[here] = own_ref[...]
+        yield True
+        copy.wait_recv()
+
+        def project(i, carry):
+            cols = pl.ds(pl.multiple_of(i * columns, columns), columns)
+            there = pl.ds(pl.multiple_of(skip + i * columns, columns), columns)
+            do[:, cols] = jnp.dot(
+                branch_ref[...], attn_ref[:, there], preferred_element_type=jnp.float32
+            ).astype(do.dtype)
+            return carry
+
+        lax.fori_loop(0, inner // columns, project, 0)
+        yield from core.run(begin_ref, q_ref, kv_ref, lse_ref, raw_ref, do, dq_ref, dkv, delta)
+        yield from sums.run(dkv, sums_ref, *scratch)
+        copy.wait_send()
+
+    def targets():
+        return [("half", True, {"dp": lax.axis_index("dp"), "head": 1 - lax.axis_index("head")})] + sums.targets()
+
+    return Task(
+        [begin, q, kv, lse, raw, own, attn],
+        [VMEM] * 7,
+        [d_query] + sums.outs + [jax.ShapeDtypeStruct((tokens, width), jnp.bfloat16)],
+        [VMEM] * 3,
+        core.scratch
+        + [pltpu.VMEM(q.shape, jnp.bfloat16), pltpu.VMEM(d_kv.shape, d_kv.dtype), dma, dma]
+        + sums.scratch,
+        targets,
+        run,
+    )
+
+
+def weight_grads(rows, grads, d_gate, d_up, active):
+    arrays = [rows, grads, d_gate, d_up, active]
+    width, units = rows.shape[1], active.shape[1]
+    columns = 256
+    down = (((0,), (0,)), ((), ()))
+
+    def run(*refs):
+        ins, (o_ref,), held, (sems,) = refs[:5], refs[5:6], refs[6:11], refs[11:]
+        copies = [pltpu.make_async_copy(ins[i], held[i], sems.at[i]) for i in range(5)]
+        for i in (0, 2, 3, 1, 4):
+            copies[i].start()
+        yield True
+        for i in (0, 2, 3):
+            copies[i].wait()
+
+        def first(i, carry):
+            cols = pl.ds(pl.multiple_of(i * columns, columns), columns)
+            for kind in (0, 1):
+                o_ref[kind, cols] = lax.dot_general(
+                    held[0][:, cols], held[2 + kind][...], down, preferred_element_type=jnp.float32
+                ).astype(o_ref.dtype)
+            return carry
+
+        def second(i, carry):
+            cols = pl.ds(pl.multiple_of(i * columns, columns), columns)
+            o_ref[2, cols] = lax.dot_general(
+                held[1][:, cols], held[4][...], down, preferred_element_type=jnp.float32
+            ).astype(o_ref.dtype)
+            return carry
+
+        lax.fori_loop(0, width // columns, first, 0)
+        yield True
+        for i in (1, 4):
+            copies[i].wait()
+        lax.fori_loop(0, width // columns, second, 0)
+        yield True
+
+    return Task(
+        arrays,
+        [HBM] * 5,
+        [jax.ShapeDtypeStruct((3, width, units), jnp.bfloat16)],
+        [VMEM],
+        [pltpu.VMEM(a.shape, a.dtype) for a in arrays] + [dma((5,))],
+        None,
+        run,
+    )
 
 
 def longest(token_count):
@@ -923,17 +1086,17 @@
     begin = doc_begin[:, None].astype(jnp.int32)
     most = longest(count * tok_rows)
     mlp_local = jnp.stack([gate_weight, up_weight, down_weight.T])
-    ((attended_raw, row_lse), (mlp_full,)) = fuse(
-        3, "attend_spread", attend(most, begin, query_rows, kv_all), spread(mlp_local, count)
+    gain_two = gain_mlp.astype(f32)
+    ahead = (0, 1) + (1, 1, 1, 0) + (1, 1, 1, 0) + (1, 0, 1, 1, 0) + (1,) * 6 + (0,)
+    ((mlp_full,), (attended_raw, row_lse, hidden, rows_all)) = fuse(
+        3,
+        "forward_spread",
+        spread(mlp_local, count),
+        forward(most, count, begin, query_rows, kv_all, attn_full, mine(layer_in), gain_two[None, :]),
+        order=ahead,
     )
     attended = attended_raw.astype(bf16)
-    branch_part = dot(attended, full_o, across_dims)
-    ((branch_peer,),) = fuse(4, "swap_branch", swap([other(branch_part).astype(bf16)]))
-    hidden = mine(inputs) + (mine(branch_part) + branch_peer.astype(f32))
     scale_two = rms_scale(hidden)
-    gain_two = gain_mlp.astype(f32)
-    normed_mlp = (hidden * scale_two * gain_two).astype(bf16)
-    ((rows_all,),) = fuse(5, "gather_rows", gather(normed_mlp, count, tower=True))
     rows_all = rows_all.reshape(-1, width)
 
     full_gate, full_up, full_down = mlp_full[0], mlp_full[1], mlp_full[2]
@@ -947,29 +1110,36 @@
     d_up = (d_active * silu_gate).astype(bf16)
     mlp_part = dot(active, full_down, across_dims).astype(bf16)
     norm_two_part = (dot(d_gate, full_gate, across_dims) + dot(d_up, full_up, across_dims)).astype(bf16)
-    mlp_grads = jnp.stack(
-        [
-            dot(rows_all, d_gate, token_dims).astype(bf16),
-            dot(rows_all, d_up, token_dims).astype(bf16),
-            dot(grad_all, active, token_dims).astype(bf16),
-        ]
-    )
-    d_normed_mlp = scatter_all(norm_two_part, count, 8, "scatter_rows", tower=True)
+    operands = (rows_all, grad_all, d_gate, d_up, active)
+    if count <= 16:
+        ((d_normed_mlp,), (mlp_grads,)) = fuse(
+            8,
+            "scatter_grads",
+            scatter(norm_two_part, count, tower=True),
+            weight_grads(*operands),
+            order=(0, 1, 0, 0, 0, 1, 0, 0, 1),
+        )
+    else:
+        d_normed_mlp = scatter_all(norm_two_part, count, 8, "scatter_rows", tower=True)
+        mlp_grads = jnp.stack(
+            [
+                dot(rows_all, d_gate, token_dims).astype(bf16),
+                dot(rows_all, d_up, token_dims).astype(bf16),
+                dot(grad_all, active, token_dims).astype(bf16),
+            ]
+        )
     gain_two_local = jnp.sum(d_normed_mlp * hidden * scale_two, axis=0)
     d_hidden = cotangent + norm_back(d_normed_mlp, hidden, scale_two, gain_two)
     branch_own = d_hidden.astype(bf16)
-    ((branch_peer,),) = fuse(16, "swap_grad", swap([branch_own]))
-    branch_grad = join(branch_own, branch_peer)
+    ((mlp_part_sums,), (d_query, kv_sums, branch_grad)) = fuse(
+        17,
+        "backward_collect",
+        collect(mlp_grads, count, ff_cols),
+        backward(most, count, begin, query_rows, kv_all, row_lse, attended_raw, branch_own, attn_full),
+        order=(1, 0, 1, 1, 0, 1, 0, 1, 0, 1, 1, 0),
+    )
+    mlp_part_sums = mlp_part_sums.astype(f32)
     out_proj_grad = dot(branch_grad, attended, token_dims)
-    d_attended = dot(branch_grad, full_o).astype(bf16)
-    ((d_query, d_kv), (mlp_part_sums,)) = fuse(
-        17,
-        "attend_back_collect",
-        attend_back(most, begin, query_rows, kv_all, row_lse, attended_raw, d_attended),
-        collect(mlp_grads, count, ff_cols),
-    )
-    mlp_part_sums = mlp_part_sums.astype(f32)
-    kv_sums = scatter_all(d_kv, count, 18, "scatter_keys")
     d_queries = (d_query * SCALE).astype(bf16).astype(f32)
     d_key_rot = kv_sums[:, :kv_cols].astype(bf16).astype(f32)
     d_value_rows = kv_sums[:, kv_cols:].astype(bf16)

time: 695 us -> 618 us (0.89)
  Pallas kernels: 538 us -> 486 us
  matrix products: 82.3 us -> 62.6 us
    pallas_call x11 -> x7, Pallas kernels: 538 us -> 486 us  [fuse(): pl.pallas_call(kernel, out_shape=[o for t in tasks for o in t.outs], in_s...]
    dot_general x15 -> x10, matrix products: 82.3 us -> 62.6 us  [dot(): lax.dot_general(a, b, (dims, ((), ())), preferred_element_type=jnp.float32)]
where the time goes in v2:
time: 618 us; the launch traced here: 610 us
  Pallas kernels  486 us (79%)
  matrix products  62.6 us (10%)
  other arithmetic  37.5 us (6%)
  local copies, waits for them, and re-layouts  22.3 us (4%)
    pallas_call x7, Pallas kernels, fuse(): pl.pallas_call(kernel, out_shape=[o for t in tasks for o in t.outs], in_s...  486 us
    dot_general x10, matrix products, dot(): lax.dot_general(a, b, (dims, ((), ())), preferred_element_type=jnp.float32)  62.6 us

profile of v2, /device:TPU:1, one launch (start us, length us, event | category | flops | bytes accessed | tf_op | source)
XLA Modules:
  0.0 610.5 jit_solution(16222053817652596037)
XLA Ops:
  0.7 0.8 select_reduce_fusion
  1.5 0.5 copy-done.28
  2.0 1.9 fusion.25.refs_1_
  3.9 1.8 maximum_bitcast_fusion.refs_0_
  5.7 67.4 %gather_inputs.1 = (bf16[16,1,96,1792]{3,2,1,0:T(8,128)(2,1)}, bf16[16,1,128,1536]{3,2,1,0:T(8,128)(2,1)}) custom-call(bf16[1,96,1792]{2,1,0:T(8,128)(2,1)} %maximum_bitcast_fusion.refs_0_, bf16[1,128,1536]{2,1,0:T(8,128)(2,1)} %fusion.25.refs_1_), custom_call_target="tpu_custom_call" | custom-call | tf_op jit(solution)/shard_map/gather_inputs/pallas_call | solution.py:125
  73.1 0.7 convert_element_type.96
  73.8 1.4 multiply_reduce_fusion
  75.2 0.7 maximum_convert_fusion.1
  75.9 3.2 fusion.21
  79.1 1.0 copy-done.6
  81.1 1.1 fusion.28
  82.3 0.6 copy-done.15
  83.2 1.0 mul.239
  84.2 0.3 copy.39
  84.5 1.4 add_convert_fusion.2
  85.9 1.0 fusion.29
  86.9 0.7 pad_maximum_fusion.7.refs_0_
  87.6 24.3 %gather_keys.1 = bf16[16,1,256,256]{3,2,1,0:T(8,128)(2,1)} custom-call(bf16[1,256,256]{2,1,0:T(8,128)(2,1)} %pad_maximum_fusion.7.refs_0_), custom_call_target="tpu_custom_call" | custom-call | tf_op jit(solution)/shard_map/gather_keys/pallas_call | solution.py:125
  111.9 0.8 slice.127.refs_2_
  112.7 0.8 constant_dynamic-slice_fusion.refs_5_
  113.5 0.8 copy.42.refs_1_
  114.3 3.0 pad_maximum_fusion.1.refs_0_
  117.3 0.6 broadcast_in_dim.30.refs_6_
  117.9 113.2 %forward_spread.1 = (bf16[3,1536,640]{2,1,0:T(8,128)(2,1)}, f32[256,768]{1,0:T(8,128)}, f32[256,128]{1,0:T(8,128)}, f32[128,1536]{1,0:T(8,128)}, bf16[16,1,128,1536]{3,2,1,0:T(8,128)(2,1)}) custom-call(bf16[3,96,4480]{2,1,0:T(8,128)(2,1)} %pad_maximum_fusion.1.refs_0_, s32[256,1]{1,0:T(8,128)} %copy.42.refs_1_, bf16[256,768]{1,0:T(8,128)(2,1)} %slice.127.refs_2_, ...), custom_call_target="tpu_custom_call" | custom-call | tf_op jit(solution)/shard_map/forward_spread/pallas_call | solution.py:125
  231.1 9.4 %fusion.13 = f32[2048,640]{1,0:T(8,128)} fusion(bf16[2048,1536]{1,0:T(8,128)(2,1)} %bitcast.81, bf16[3,1536,640]{2,1,0:T(8,128)(2,1)} %get-tuple-element.36), kind=kOutput, calls=%fused_computation.23 | convolution fusion | flops 4026531840 | bytes 13500416 | tf_op jit(solution)/shard_map/dot_general | solution.py:908
  240.5 6.8 %fusion.7 = f32[2048,640]{1,0:T(8,128)} fusion(bf16[2048,1536]{1,0:T(8,128)(2,1)S(1)} %bitcast.84, bf16[3,1536,640]{2,1,0:T(8,128)(2,1)S(1)} %copy-done.30), kind=kOutput, calls=%fused_computation.17 | convolution fusion | flops 4026531840 | bytes 13500416 | tf_op jit(solution)/shard_map/dot_general | solution.py:908
  247.3 10.1 %multiply_convert_fusion = (bf16[2048,640]{1,0:T(8,128)(2,1)}, bf16[2048,640]{1,0:T(8,128)(2,1)S(1)}, bf16[2048,640]{1,0:T(8,128)(2,1)S(1)}) fusion(f32[2048,640]{1,0:T(8,128)} %fusion.7, f32[2048,640]{1,0:T(8,128)} %fusion.13, bf16[2048,1536]{1,0:T(8,128)(2,1)S(1)} %bitcast.85, bf16[3,1536,640]{2,1,0:T(8,128)(2,1)S(1)} %copy-done.30), kind=kOutput, calls=%fused_computation.3 | convolution fusion | flops 4046192640 | bytes 26607616 | tf_op jit(solution)/shard_map/dot_general | solution.py:908
  257.5 8.1 %fusion.5 = f32[2048,1536]{1,0:T(8,128)} fusion(bf16[2048,640]{1,0:T(8,128)(2,1)S(1)} %get-tuple-element.61.refs_3_, bf16[3,1536,640]{2,1,0:T(8,128)(2,1)S(1)} %copy-done.30), kind=kOutput, calls=%fused_computation.15 | convolution fusion | flops 4026531840 | bytes 17170432 | tf_op jit(solution)/shard_map/dot_general | solution.py:908
  265.6 10.3 %add_convert_fusion = bf16[2048,1536]{1,0:T(8,128)(2,1)} fusion(f32[2048,1536]{1,0:T(8,128)} %fusion.5, bf16[2048,640]{1,0:T(8,128)(2,1)S(1)} %get-tuple-element.62.refs_4_, bf16[3,1536,640]{2,1,0:T(8,128)(2,1)S(1)} %copy-done.30), kind=kOutput, calls=%fused_computation | convolution fusion | flops 4032823296 | bytes 23461888 | tf_op jit(solution)/shard_map/dot_general | solution.py:908
  276.0 54.4 %scatter_grads.1 = (f32[128,1536]{1,0:T(8,128)}, bf16[3,1536,640]{2,1,0:T(8,128)(2,1)}) custom-call(bf16[16,128,1536]{2,1,0:T(8,128)(2,1)} %bitcast.86, bf16[2048,1536]{1,0:T(8,128)(2,1)} %bitcast.83, bf16[2048,1536]{1,0:T(8,128)(2,1)} %bitcast.82, bf16[2048,640]{1,0:T(8,128)(2,1)} %copy-done.10, bf16[2048,640]{1,0:T(8,128)(2,1)} %copy-done.11, ...), custom_call_target="tpu_custom_call" | custom-call | tf_op jit(solution)/shard_map/scatter_grads/pallas_call | solution.py:125
  330.6 1.3 multiply_reduce_fusion.4
  332.0 2.5 fusion.33
  334.4 105.5 %backward_collect.1 = (bf16[3,96,4480]{2,1,0:T(8,128)(2,1)}, f32[256,768]{1,0:T(8,128)}, f32[256,256]{1,0:T(8,128)}, bf16[256,1536]{1,0:T(8,128)(2,1)}) custom-call(bf16[3,1536,640]{2,1,0:T(8,128)(2,1)} %get-tuple-element.38.refs_0_, s32[256,1]{1,0:T(8,128)} %copy.42.refs_1_, bf16[256,768]{1,0:T(8,128)(2,1)} %slice.127.refs_2_, bf16[4096,256]{1,0:T(8,128)(2,1)} %bitcast.78, ...), custom_call_target="tpu_custom_call" | custom-call | tf_op jit(solution)/shard_map/backward_collect/pallas_call | solution.py:125
  440.0 1.2 multiply_convert_fusion.4
  441.2 1.1 convert.26
  442.3 0.6 fusion.36
  443.0 0.6 copy-done.22
  443.6 1.0 maximum_convert_fusion
  444.6 1.5 copy.45
  446.3 1.2 copy.46
  447.6 1.4 add_convert_fusion.1
  449.0 4.1 fusion.1
  453.0 1.9 dynamic-slice_convert_fusion.refs_2_
  455.0 1.1 convolution_convert_fusion.1
  456.3 0.8 convolution_convert_fusion.2
  457.2 2.9 pad_maximum_fusion.refs_0_
  460.1 8.5 %convolution_convert_fusion = bf16[2048,1536]{1,0:T(8,128)(2,1)} fusion(bf16[2048,640]{1,0:T(8,128)(2,1)S(1)} %copy-done.9, bf16[3,1536,640]{2,1,0:T(8,128)(2,1)} %get-tuple-element.36), kind=kOutput, calls=%fused_computation.1 | convolution fusion | flops 4029677568 | bytes 10878976 | tf_op jit(solution)/shard_map/dot_general | solution.py:908
  468.7 70.6 %scatter_last.1 = (f32[96,1792]{1,0:T(8,128)}, f32[128,1536]{1,0:T(8,128)}, bf16[128,1536]{1,0:T(8,128)(2,1)}) custom-call(bf16[16,96,1792]{2,1,0:T(8,128)(2,1)} %pad_maximum_fusion.refs_0_, bf16[16,128,1536]{2,1,0:T(8,128)(2,1)} %bitcast.80, bf16[128,1536]{1,0:T(8,128)(2,1)} %dynamic-slice_convert_fusion.refs_2_), custom_call_target="tpu_custom_call" | custom-call | tf_op jit(solution)/shard_map/scatter_last/pallas_call | solution.py:125
  539.3 2.1 add_convert_fusion.4.refs_2_
  542.0 1.0 add_convert_fusion.3.refs_1_
  543.1 0.6 maximum_bitcast_fusion.1.refs_0_
  543.8 51.0 %gather_sums.1 = (f32[16,2,32,128]{3,2,1,0:T(8,128)}, bf16[128,1536]{1,0:T(8,128)(2,1)}, bf16[128,1536]{1,0:T(8,128)(2,1)}) custom-call(f32[1,32,128]{2,1,0:T(8,128)} %maximum_bitcast_fusion.1.refs_0_, bf16[128,1536]{1,0:T(8,128)(2,1)} %add_convert_fusion.3.refs_1_, bf16[128,1536]{1,0:T(8,128)(2,1)} %add_convert_fusion.4.refs_2_), custom_call_target="tpu_custom_call" | custom-call | tf_op jit(solution)/shard_map/gather_sums/pallas_call | solution.py:125
  594.8 2.3 reshape.290
  597.1 1.2 slice_reduce_fusion
  598.2 1.2 slice_reduce_fusion.1
  599.5 0.6 fusion.38
  600.1 2.3 maximum_select_fusion.1
  602.3 2.3 maximum_select_fusion
  604.6 0.6 slice.138
  605.2 0.5 fusion.37
  605.7 0.8 slice_bitcast_fusion.3
  606.6 0.6 fusion.35
  607.2 0.3 convert_element_type.118
  607.6 2.4 slice_bitcast_fusion
  (88 shorter events, 2.9 us)
Async XLA Ops:
  1.5 0.5 copy-start.28
  75.2 3.9 copy-start.26
  79.1 1.0 copy-start.6
  80.1 0.7 copy-start.31
  82.2 0.7 copy-start.15
  84.5 28.2 %copy-start.2 = (bf16[256,1536]{1,0:T(8,128)(2,1)S(1)}, bf16[256,1536]{1,0:T(8,128)(2,1)}, u32[]{:S(2)}) copy-start(bf16[256,1536]{1,0:T(8,128)(2,1)} %param.17) | copy-start | bytes 2359300
  84.5 29.8 %copy-start.17 = (bf16[4480,96]{0,1:T(8,128)(2,1)S(1)}, bf16[4480,96]{0,1:T(8,128)(2,1)}, u32[]{:S(2)}) copy-start(bf16[4480,96]{0,1:T(8,128)(2,1)} %param.29) | copy-start | bytes 2580484
  85.9 28.4 %copy-start.18 = (bf16[96,4480]{1,0:T(8,128)(2,1)S(1)}, bf16[96,4480]{1,0:T(8,128)(2,1)}, u32[]{:S(2)}) copy-start(bf16[96,4480]{1,0:T(8,128)(2,1)} %param.28) | copy-start | bytes 2580484
  112.7 4.6 copy-start.25
  231.1 9.4 %copy-start.1 = (bf16[16,1,128,1536]{3,2,1,0:T(8,128)(2,1)S(1)}, bf16[16,1,128,1536]{3,2,1,0:T(8,128)(2,1)}, u32[]{:S(2)}) copy-start(bf16[16,1,128,1536]{3,2,1,0:T(8,128)(2,1)} %get-tuple-element.37) | copy-start | bytes 18874372
  231.1 9.4 %copy-start.30 = (bf16[3,1536,640]{2,1,0:T(8,128)(2,1)S(1)}, bf16[3,1536,640]{2,1,0:T(8,128)(2,1)}, u32[]{:S(2)}) copy-start(bf16[3,1536,640]{2,1,0:T(8,128)(2,1)} %get-tuple-element.36) | copy-start | bytes 17694724
  257.5 8.2 %copy-start.10 = (bf16[2048,640]{1,0:T(8,128)(2,1)}, bf16[2048,640]{1,0:T(8,128)(2,1)S(1)}, u32[]{:S(2)}) copy-start(bf16[2048,640]{1,0:T(8,128)(2,1)S(1)} %get-tuple-element.61.refs_3_) | copy-start | bytes 7864324
  257.5 8.2 %copy-start.11 = (bf16[2048,640]{1,0:T(8,128)(2,1)}, bf16[2048,640]{1,0:T(8,128)(2,1)S(1)}, u32[]{:S(2)}) copy-start(bf16[2048,640]{1,0:T(8,128)(2,1)S(1)} %get-tuple-element.62.refs_4_) | copy-start | bytes 7864324
  276.0 54.4 %copy-start = (f32[128,1536]{1,0:T(8,128)S(1)}, f32[128,1536]{1,0:T(8,128)}, u32[]{:S(2)}) copy-start(f32[128,1536]{1,0:T(8,128)} %get-tuple-element.34) | copy-start | bytes 2359300
  276.0 56.0 %copy-start.19 = (bf16[256,1536]{1,0:T(8,128)(2,1)S(1)}, bf16[256,1536]{1,0:T(8,128)(2,1)}, u32[]{:S(2)}) copy-start(bf16[256,1536]{1,0:T(8,128)(2,1)} %param.33) | copy-start | bytes 2359300
  276.0 55.9 %copy-start.29 = (f32[128]{0:T(128)S(1)}, f32[128]{0:T(128)}, u32[]{:S(2)}) copy-start(f32[128]{0:T(128)} %copy-done.28) | copy-start | bytes 1540
  440.0 6.1 %copy-start.16 = (f32[256,128]{0,1:T(8,128)S(1)}, f32[256,128]{0,1:T(8,128)}, u32[]{:S(2)}) copy-start(f32[256,128]{0,1:T(8,128)} %copy-done.15) | copy-start | bytes 393220
  441.2 1.8 copy-start.5
  443.0 0.6 copy-start.22
  446.2 1.4 copy-start.23
  446.2 2.7 copy-start.24
  449.0 6.0 copy-start.27
  455.0 1.1 copy-start.8
  455.0 1.4 copy-start.20
  457.2 2.9 copy-start.9
  539.3 2.4 copy-start.13
  539.3 2.4 copy-start.14
  539.3 2.7 copy-start.7
  542.0 60.4 %copy-start.3 = (bf16[128,1536]{1,0:T(8,128)(2,1)S(1)}, bf16[128,1536]{1,0:T(8,128)(2,1)}, u32[]{:S(2)}) copy-start(bf16[128,1536]{1,0:T(8,128)(2,1)} %add_convert_fusion.4.refs_2_) | copy-start | bytes 1179652
  543.0 57.1 %copy-start.4 = (bf16[128,1536]{1,0:T(8,128)(2,1)S(1)}, bf16[128,1536]{1,0:T(8,128)(2,1)}, u32[]{:S(2)}) copy-start(bf16[128,1536]{1,0:T(8,128)(2,1)} %add_convert_fusion.3.refs_1_) | copy-start | bytes 1179652
  594.8 12.4 %copy-start.12 = (bf16[3,96,4480]{2,1,0:T(8,128)(2,1)S(1)}, bf16[3,96,4480]{2,1,0:T(8,128)(2,1)}, u32[]{:S(2)}) copy-start(bf16[3,96,4480]{2,1,0:T(8,128)(2,1)} %get-tuple-element.51) | copy-start | bytes 7741444
  600.1 5.6 copy-start.21

commit v3 on v2

--- a/solution.py
+++ b/solution.py
@@ -260,7 +260,8 @@
         row, col, core = grid.row, grid.col, grid.core
         found = [(("hop", tower, 4), True, grid.where(row, col, 1 - core))]
         found += [(("col", tower, e), True, grid.where(row, (col + e) % across, core)) for e in range(1, across)]
-        found += [(("row", tower, d), True, grid.where((row + d) % lines, col, core)) for d in range(1, lines)]
+        found.append((("hop", tower, 0), row < lines - 1, grid.where(row + 1, col, core)))
+        found.append((("hop", tower, 1), row > 0, grid.where(row - 1, col, core)))
         return found
 
     def run(x_ref, o_ref, near, first, wide, second, far, s1, r1, s2, r2, s3, r3):
@@ -277,14 +278,19 @@
                 first.at[r, e - 1], wide.at[r, e - 1], s2.at[r, e], r2.at[r, e], grid.where(row, (col + e) % across, core)
             )
 
-        def three(d):
-            return remote(
-                second.at[d - 1], far.at[d - 1], s3.at[d], r3.at[d], grid.where((row + d) % lines, col, core)
-            )
-
-        lines_order = [d for d in range(1, lines)] + [0]
-        for d in lines_order:
-            r = (row + d) % lines
+        def three(r):
+            to = jnp.where(r > row, row + 1, row - 1)
+            place = jnp.where((r > row) | (to != r), r, lines)
+            return remote(second.at[r], far.at[place], s3.at[r], r3.at[place], grid.where(to, col, core))
+
+        def arrived(place):
+            remote(second.at[0], far.at[place], s3.at[0], r3.at[place], grid.where(row, col, 1 - core)).wait_recv()
+
+        def turn(t):
+            return jnp.where(row < lines // 2, lines - 1 - t, t)
+
+        for t in range(lines):
+            r = turn(t)
             for e in [e for e in range(1, across)] + [0]:
                 one(r, (col + e) % across).start()
         yield True
@@ -296,8 +302,8 @@
 
             lax.fori_loop(0, height // step, run_block, 0)
 
-        for d in lines_order:
-            r = (row + d) % lines
+        for t in range(lines):
+            r = turn(t)
             for e in range(1, across):
                 q = (col + e) % across
                 one(r, q).wait_recv()
@@ -310,11 +316,12 @@
                 blocks(add)
                 two(r, e).start()
             yield True
-        for d in lines_order:
-            r = (row + d) % lines
+        for t in range(lines):
+            r = turn(t)
             one(r, col).wait_recv()
             for e in range(1, across):
                 two(r, e).wait_recv()
+            behind = ((r > row) & (row > 0)) | ((r < row) & (row < lines - 1))
 
             def total(rows):
                 value = x_ref[grid.index(r, col, core), rows].astype(jnp.float32) + near[r, col, rows].astype(jnp.float32)
@@ -322,32 +329,53 @@
                     value = value + wide[r, e - 1, rows].astype(jnp.float32)
                 return value
 
-            if d:
-
-                def add(rows):
-                    second[d - 1, rows] = total(rows).astype(second.dtype)
-
-                blocks(add)
-                three(d).start()
-            else:
-                for e in range(1, lines):
-                    three(e).wait_recv()
-
-                def add(rows):
-                    value = total(rows)
-                    for e in range(1, lines):
-                        value = value + far[e - 1, rows].astype(jnp.float32)
-                    o_ref[rows] = value.astype(o_ref.dtype)
-
-                blocks(add)
+            @pl.when(r == row)
+            def _():
+                def keep(rows):
+                    o_ref[rows] = total(rows).astype(o_ref.dtype)
+
+                blocks(keep)
+
+            @pl.when((r != row) & jnp.logical_not(behind))
+            def _():
+                def begin(rows):
+                    second[r, rows] = total(rows).astype(second.dtype)
+
+                blocks(begin)
+                three(r).start()
+
+            @pl.when((r != row) & behind)
+            def _():
+                arrived(r)
+
+                def pass_on(rows):
+                    second[r, rows] = (total(rows) + far[r, rows].astype(jnp.float32)).astype(second.dtype)
+
+                blocks(pass_on)
+                three(r).start()
+
             yield True
+        for ok, place in ((row > 0, row), (row < lines - 1, lines)):
+
+            @pl.when(ok)
+            def _():
+                arrived(place)
+
+                def last(rows):
+                    o_ref[rows] = (o_ref[rows] + far[place, rows].astype(jnp.float32)).astype(o_ref.dtype)
+
+                blocks(last)
+
+        yield True
         for r in range(lines):
             for q in range(across):
                 one(r, q).wait_send()
             for e in range(1, across):
                 two(r, e).wait_send()
-        for d in range(1, lines):
-            three(d).wait_send()
+
+            @pl.when(r != row)
+            def _():
+                three(r).wait_send()
 
     return Task(
         [x],
@@ -358,14 +386,14 @@
             pltpu.VMEM((lines, across) + block, x.dtype),
             pltpu.VMEM((lines, across - 1) + block, x.dtype),
             pltpu.VMEM((lines, across - 1) + block, x.dtype),
-            pltpu.VMEM((lines - 1,) + block, x.dtype),
-            pltpu.VMEM((lines - 1,) + block, x.dtype),
+            pltpu.VMEM((lines,) + block, x.dtype),
+            pltpu.VMEM((lines + 1,) + block, x.dtype),
             dma((lines, across)),
             dma((lines, across)),
             dma((lines, across)),
             dma((lines, across)),
             dma((lines,)),
-            dma((lines,)),
+            dma((lines + 1,)),
         ],
         targets,
         run,
@@ -963,17 +991,31 @@
     )
 
 
-def weight_grads(rows, grads, d_gate, d_up, active):
-    arrays = [rows, grads, d_gate, d_up, active]
-    width, units = rows.shape[1], active.shape[1]
+def weight_grads(rows, grads, d_gate, d_up, active, weights):
+    arrays = [rows, grads, d_gate, d_up, active, weights]
+    width, units, tokens = rows.shape[1], active.shape[1], rows.shape[0]
     columns = 256
     down = (((0,), (0,)), ((), ()))
+    across = (((1,), (1,)), ((), ()))
 
     def run(*refs):
-        ins, (o_ref,), held, (sems,) = refs[:5], refs[5:6], refs[6:11], refs[11:]
-        copies = [pltpu.make_async_copy(ins[i], held[i], sems.at[i]) for i in range(5)]
-        for i in (0, 2, 3, 1, 4):
+        ins, (o_ref, out_ref), held, (sems,) = refs[:6], refs[6:8], refs[8:14], refs[14:]
+        sources = list(ins[:5]) + [ins[5].at[2]]
+        copies = [pltpu.make_async_copy(sources[i], held[i], sems.at[i]) for i in range(6)]
+        for i in (4, 5, 0, 2, 3, 1):
             copies[i].start()
+        yield True
+        for i in (4, 5):
+            copies[i].wait()
+
+        def forth(i, carry):
+            here = pl.ds(pl.multiple_of(i * columns, columns), columns)
+            out_ref[here] = lax.dot_general(
+                held[4][here], held[5][...], across, preferred_element_type=jnp.float32
+            ).astype(out_ref.dtype)
+            return carry
+
+        lax.fori_loop(0, tokens // columns, forth, 0)
         yield True
         for i in (0, 2, 3):
             copies[i].wait()
@@ -993,19 +1035,21 @@
             ).astype(o_ref.dtype)
             return carry
 
-        lax.fori_loop(0, width // columns, first, 0)
-        yield True
-        for i in (1, 4):
-            copies[i].wait()
+        half = width // columns // 2
+        lax.fori_loop(0, half, first, 0)
+        yield True
+        lax.fori_loop(half, width // columns, first, 0)
+        yield True
+        copies[1].wait()
         lax.fori_loop(0, width // columns, second, 0)
         yield True
 
     return Task(
         arrays,
-        [HBM] * 5,
-        [jax.ShapeDtypeStruct((3, width, units), jnp.bfloat16)],
-        [VMEM],
-        [pltpu.VMEM(a.shape, a.dtype) for a in arrays] + [dma((5,))],
+        [HBM] * 6,
+        [jax.ShapeDtypeStruct((3, width, units), jnp.bfloat16), jax.ShapeDtypeStruct((tokens, width), jnp.bfloat16)],
+        [VMEM] * 2,
+        [pltpu.VMEM(a.shape, a.dtype) for a in arrays[:5]] + [pltpu.VMEM((width, units), weights.dtype), dma((6,))],
         None,
         run,
     )
@@ -1062,11 +1106,8 @@
         jnp.sum(jnp.where(picked, source_weights[None, :], 0), axis=1).astype(f32) / loss_denominator
     )
     cotangent = mine(out_grad).astype(f32) * mine(row_scale[:, None])
-    ((attn_full,), (grad_all,)) = fuse(
-        1, "gather_inputs", gather(attn_local, count), gather(cotangent.astype(bf16), count, tower=True)
-    )
+    ((attn_full,),) = fuse(1, "gather_weights", gather(attn_local, count))
     attn_full = attn_full.reshape(width, -1)
-    grad_all = grad_all.reshape(-1, width)
     qkv_cols = q_cols + 2 * kv_cols
     full_qkv = attn_full[:, :qkv_cols]
     full_o = attn_full[:, qkv_cols:]
@@ -1081,7 +1122,10 @@
     ).reshape(tok_rows, q_cols + kv_cols)
     query_rows = turned[:, :q_cols].astype(bf16)
     kv_rows = jnp.concatenate([turned[:, q_cols:], pre[:, q_cols + kv_cols :]], axis=1).astype(bf16)
-    ((kv_all,),) = fuse(2, "gather_keys", gather(kv_rows, count))
+    ((kv_all,), (grad_all,)) = fuse(
+        2, "gather_keys", gather(kv_rows, count), gather(cotangent.astype(bf16), count, tower=True)
+    )
+    grad_all = grad_all.reshape(-1, width)
     kv_all = kv_all.reshape(-1, 2 * kv_cols)
     begin = doc_begin[:, None].astype(jnp.int32)
     most = longest(count * tok_rows)
@@ -1108,19 +1152,19 @@
     d_active = dot(grad_all, full_down)
     d_gate = (d_active * up_act * sigmoid_gate * (1.0 + gate_act * (1.0 - sigmoid_gate))).astype(bf16)
     d_up = (d_active * silu_gate).astype(bf16)
-    mlp_part = dot(active, full_down, across_dims).astype(bf16)
     norm_two_part = (dot(d_gate, full_gate, across_dims) + dot(d_up, full_up, across_dims)).astype(bf16)
-    operands = (rows_all, grad_all, d_gate, d_up, active)
+
     if count <= 16:
-        ((d_normed_mlp,), (mlp_grads,)) = fuse(
+        ((d_normed_mlp,), (mlp_grads, mlp_part)) = fuse(
             8,
             "scatter_grads",
             scatter(norm_two_part, count, tower=True),
-            weight_grads(*operands),
-            order=(0, 1, 0, 0, 0, 1, 0, 0, 1),
+            weight_grads(rows_all, grad_all, d_gate, d_up, active, mlp_full),
+            order=(0, 1, 0, 0, 1, 0, 0, 1, 0, 1, 0, 1),
         )
     else:
         d_normed_mlp = scatter_all(norm_two_part, count, 8, "scatter_rows", tower=True)
+        mlp_part = dot(active, full_down, across_dims).astype(bf16)
         mlp_grads = jnp.stack(
             [
                 dot(rows_all, d_gate, token_dims).astype(bf16),
@@ -1131,13 +1175,18 @@
     gain_two_local = jnp.sum(d_normed_mlp * hidden * scale_two, axis=0)
     d_hidden = cotangent + norm_back(d_normed_mlp, hidden, scale_two, gain_two)
     branch_own = d_hidden.astype(bf16)
-    ((mlp_part_sums,), (d_query, kv_sums, branch_grad)) = fuse(
-        17,
-        "backward_collect",
+    tasks = [
         collect(mlp_grads, count, ff_cols),
         backward(most, count, begin, query_rows, kv_all, row_lse, attended_raw, branch_own, attn_full),
-        order=(1, 0, 1, 1, 0, 1, 0, 1, 0, 1, 1, 0),
-    )
+    ]
+    turns = (1, 0, 1, 1, 0, 1, 0, 1, 0, 1, 1, 0)
+    if count <= 16:
+        tasks.append(scatter(mlp_part, count, tower=True))
+        turns = (1, 0) + (2,) * 5 + (1, 0, 1, 2, 0, 1, 2, 0, 1, 2, 0, 1) + (1,) * 4 + (0, 2)
+    found = fuse(17, "backward_collect", *tasks, order=turns)
+    ((mlp_part_sums,), (d_query, kv_sums, branch_grad)) = found[:2]
+    mlp_out = found[2][0] if count <= 16 else scatter_all(mlp_part, count, 25, "scatter_out", tower=True)
+    layer_out_own = (hidden + mlp_out).astype(bf16)
     mlp_part_sums = mlp_part_sums.astype(f32)
     out_proj_grad = dot(branch_grad, attended, token_dims)
     d_queries = (d_query * SCALE).astype(bf16).astype(f32)
@@ -1156,15 +1205,12 @@
     attn_grads = jnp.concatenate([qkv_grad, out_proj_grad], axis=1).astype(bf16)
     norm_one_part = dot(d_pre, full_qkv, across_dims)
     norm_send = other(norm_one_part).astype(bf16)
+    exchange = swap([norm_send, layer_out_own])
     if count <= 16:
-        ((attn_part,), (mlp_out,), (norm_peer,)) = fuse(
-            21, "scatter_last", scatter(attn_grads, count), scatter(mlp_part, count, tower=True), swap([norm_send])
-        )
+        ((attn_part,), (norm_peer, layer_out_peer)) = fuse(21, "scatter_last", scatter(attn_grads, count), exchange)
     else:
         attn_part = scatter_all(attn_grads, count, 21, "scatter_attn")
-        mlp_out = scatter_all(mlp_part, count, 25, "scatter_out", tower=True)
-        ((norm_peer,),) = fuse(33, "swap_norm", swap([norm_send]))
-    layer_out_own = (hidden + mlp_out).astype(bf16)
+        ((norm_peer, layer_out_peer),) = fuse(33, "swap_norm", exchange)
     d_normed = mine(norm_one_part) + norm_peer.astype(f32)
     inputs_own = mine(inputs)
     scale_own = mine(scale_one)
@@ -1172,8 +1218,8 @@
     layer_in_grad_own = (d_hidden + norm_back(d_normed, inputs_own, scale_own, gain_one)).astype(bf16)
 
     small = jnp.concatenate([bias_local, gain_one_local, gain_two_local]).reshape(-1, LANES)
-    ((small_all,), (layer_in_grad_peer, layer_out_peer)) = fuse(
-        34, "gather_sums", gather(small, count, both=True), swap([layer_in_grad_own, layer_out_own])
+    ((small_all,), (layer_in_grad_peer,)) = fuse(
+        34, "gather_sums", gather(small, count, both=True), swap([layer_in_grad_own])
     )
     small_all = small_all.reshape(count, 2, -1)
     small_sum = jnp.sum(small_all[:, 0], axis=0)

time: 618 us -> 584 us (0.945)
  Pallas kernels: 486 us -> 470 us
  matrix products: 62.6 us -> 53.6 us
    pallas_call x7, Pallas kernels: 486 us -> 470 us  [fuse(): pl.pallas_call(kernel, out_shape=[o for t in tasks for o in t.outs], in_s...]
    dot_general x10 -> x9, matrix products: 62.6 us -> 53.6 us  [dot(): lax.dot_general(a, b, (dims, ((), ())), preferred_element_type=jnp.float32)]
where the time goes in v3:
time: 584 us; the launch traced here: 576 us
  Pallas kernels  470 us (80%)
  matrix products  53.6 us (9%)
  other arithmetic  32.9 us (6%)
  local copies, waits for them, and re-layouts  18.4 us (3%)
    pallas_call x7, Pallas kernels, fuse(): pl.pallas_call(kernel, out_shape=[o for t in tasks for o in t.outs], in_s...  470 us
    dot_general x9, matrix products, dot(): lax.dot_general(a, b, (dims, ((), ())), preferred_element_type=jnp.float32)  53.6 us

profile of v3, /device:TPU:1, one launch (start us, length us, event | category | flops | bytes accessed | tf_op | source)
XLA Modules:
  0.0 576.3 jit_solution(1315642715775708890)
XLA Ops:
  0.7 1.8 maximum_bitcast_fusion.refs_0_
  2.5 42.1 %gather_weights.1 = bf16[16,1,96,1792]{3,2,1,0:T(8,128)(2,1)} custom-call(bf16[1,96,1792]{2,1,0:T(8,128)(2,1)} %maximum_bitcast_fusion.refs_0_), custom_call_target="tpu_custom_call" | custom-call | tf_op jit(solution)/shard_map/gather_weights/pallas_call | solution.py:125
  44.7 0.2 multiply_reduce_fusion
  45.0 2.9 fusion.19
  47.9 1.0 copy-done.6
  48.9 0.3 copy.40
  49.3 0.2 copy-done.31
  49.5 0.2 reduce-window.9
  49.9 1.1 fusion.26
  51.1 0.6 copy-done.15
  51.7 0.3 copy.41
  52.0 1.0 mul.236
  53.0 0.3 copy.39
  53.3 1.3 add_convert_fusion.2
  54.6 1.0 fusion.27
  55.6 0.7 pad_maximum_fusion.7.refs_0_
  56.3 0.7 select_reduce_fusion
  57.1 1.9 fusion.23.refs_1_
  59.0 52.4 %gather_keys.1 = (bf16[16,1,256,256]{3,2,1,0:T(8,128)(2,1)}, bf16[16,1,128,1536]{3,2,1,0:T(8,128)(2,1)}) custom-call(bf16[1,256,256]{2,1,0:T(8,128)(2,1)} %pad_maximum_fusion.7.refs_0_, bf16[1,128,1536]{2,1,0:T(8,128)(2,1)} %fusion.23.refs_1_), custom_call_target="tpu_custom_call" | custom-call | tf_op jit(solution)/shard_map/gather_keys/pallas_call | solution.py:125
  111.4 0.8 slice.127.refs_2_
  112.2 0.8 constant_dynamic-slice_fusion.refs_5_
  112.9 0.8 copy.42.refs_1_
  113.7 3.3 pad_maximum_fusion.1.refs_0_
  117.0 0.6 broadcast_in_dim.30.refs_6_
  117.6 113.4 %forward_spread.1 = (bf16[3,1536,640]{2,1,0:T(8,128)(2,1)}, f32[256,768]{1,0:T(8,128)}, f32[256,128]{1,0:T(8,128)}, f32[128,1536]{1,0:T(8,128)}, bf16[16,1,128,1536]{3,2,1,0:T(8,128)(2,1)}) custom-call(bf16[3,96,4480]{2,1,0:T(8,128)(2,1)} %pad_maximum_fusion.1.refs_0_, s32[256,1]{1,0:T(8,128)} %copy.42.refs_1_, bf16[256,768]{1,0:T(8,128)(2,1)} %slice.127.refs_2_, ...), custom_call_target="tpu_custom_call" | custom-call | tf_op jit(solution)/shard_map/forward_spread/pallas_call | solution.py:125
  231.0 9.4 %fusion.12 = f32[2048,640]{1,0:T(8,128)} fusion(bf16[2048,1536]{1,0:T(8,128)(2,1)} %bitcast.78, bf16[3,1536,640]{2,1,0:T(8,128)(2,1)} %get-tuple-element.37.refs_6_), kind=kOutput, calls=%fused_computation.21 | convolution fusion | flops 4026531840 | bytes 13500416 | tf_op jit(solution)/shard_map/dot_general | solution.py:936
  240.4 6.8 %fusion.7 = f32[2048,640]{1,0:T(8,128)} fusion(bf16[2048,1536]{1,0:T(8,128)(2,1)S(1)} %bitcast.81, bf16[3,1536,640]{2,1,0:T(8,128)(2,1)S(1)} %copy-done.2), kind=kOutput, calls=%fused_computation.16 | convolution fusion | flops 4026531840 | bytes 13500416 | tf_op jit(solution)/shard_map/dot_general | solution.py:936
  247.3 10.1 %multiply_convert_fusion = (bf16[2048,640]{1,0:T(8,128)(2,1)}, bf16[2048,640]{1,0:T(8,128)(2,1)S(1)}, bf16[2048,640]{1,0:T(8,128)(2,1)S(1)}) fusion(f32[2048,640]{1,0:T(8,128)} %fusion.7, f32[2048,640]{1,0:T(8,128)} %fusion.12, bf16[2048,1536]{1,0:T(8,128)(2,1)S(1)} %bitcast.82, bf16[3,1536,640]{2,1,0:T(8,128)(2,1)S(1)} %copy-done.2), kind=kOutput, calls=%fused_computation.2 | convolution fusion | flops 4046192640 | bytes 26607616 | tf_op jit(solution)/shard_map/dot_general | solution.py:936
  257.4 8.1 %fusion.5 = f32[2048,1536]{1,0:T(8,128)} fusion(bf16[2048,640]{1,0:T(8,128)(2,1)S(1)} %get-tuple-element.63.refs_3_, bf16[3,1536,640]{2,1,0:T(8,128)(2,1)S(1)} %copy-done.2), kind=kOutput, calls=%fused_computation.14 | convolution fusion | flops 4026531840 | bytes 17170432 | tf_op jit(solution)/shard_map/dot_general | solution.py:936
  265.6 10.2 %add_convert_fusion = bf16[2048,1536]{1,0:T(8,128)(2,1)} fusion(f32[2048,1536]{1,0:T(8,128)} %fusion.5, bf16[2048,640]{1,0:T(8,128)(2,1)S(1)} %get-tuple-element.64.refs_4_, bf16[3,1536,640]{2,1,0:T(8,128)(2,1)S(1)} %copy-done.2), kind=kOutput, calls=%fused_computation | convolution fusion | flops 4032823296 | bytes 23461888 | tf_op jit(solution)/shard_map/dot_general | solution.py:936
  275.7 59.6 %scatter_grads.1 = (f32[128,1536]{1,0:T(8,128)}, bf16[3,1536,640]{2,1,0:T(8,128)(2,1)}, bf16[2048,1536]{1,0:T(8,128)(2,1)}) custom-call(bf16[16,128,1536]{2,1,0:T(8,128)(2,1)} %bitcast.83, bf16[2048,1536]{1,0:T(8,128)(2,1)} %bitcast.80, bf16[2048,1536]{1,0:T(8,128)(2,1)} %bitcast.79, bf16[2048,640]{1,0:T(8,128)(2,1)} %copy-done.9, ...), custom_call_target="tpu_custom_call" | custom-call | tf_op jit(solution)/shard_map/scatter_grads/pallas_call | solution.py:125
  335.5 1.4 multiply_reduce_fusion.1
  336.9 2.5 fusion.31
  339.3 118.5 %backward_collect.1 = (bf16[3,96,4480]{2,1,0:T(8,128)(2,1)}, f32[256,768]{1,0:T(8,128)}, f32[256,256]{1,0:T(8,128)}, bf16[256,1536]{1,0:T(8,128)(2,1)}, f32[128,1536]{1,0:T(8,128)}) custom-call(bf16[3,1536,640]{2,1,0:T(8,128)(2,1)} %get-tuple-element.39.refs_0_, s32[256,1]{1,0:T(8,128)} %copy.42.refs_1_, bf16[256,768]{1,0:T(8,128)(2,1)} %slice.127.refs_2_, ...), custom_call_target="tpu_custom_call" | custom-call | tf_op jit(solution)/shard_map/backward_collect/pallas_call | solution.py:125
  457.9 2.0 add_convert_fusion.4.refs_2_
  459.9 1.2 multiply_convert_fusion.4
  461.1 0.7 fusion.34
  461.8 0.6 copy-done.20
  462.5 0.3 copy.45
  462.8 1.0 broadcast_multiply_fusion
  464.0 0.3 copy.46
  464.3 1.2 add_convert_fusion.1
  465.5 0.8 copy-done.12
  466.2 3.0 fusion.1
  469.2 0.8 dynamic-slice_convert_fusion.refs_1_
  470.0 2.2 convolution_convert_fusion
  472.3 0.8 convolution_convert_fusion.1
  473.1 2.9 pad_maximum_fusion.refs_0_
  476.1 56.7 %scatter_last.1 = (f32[96,1792]{1,0:T(8,128)}, bf16[128,1536]{1,0:T(8,128)(2,1)}, bf16[128,1536]{1,0:T(8,128)(2,1)}) custom-call(bf16[16,96,1792]{2,1,0:T(8,128)(2,1)} %pad_maximum_fusion.refs_0_, bf16[128,1536]{1,0:T(8,128)(2,1)} %dynamic-slice_convert_fusion.refs_1_, bf16[128,1536]{1,0:T(8,128)(2,1)} %add_convert_fusion.4.refs_2_), custom_call_target="tpu_custom_call" | custom-call | tf_op jit(solution)/shard_map/scatter_last/pallas_call | solution.py:125
  533.1 1.4 multiply_reduce_fusion.3
  534.5 1.0 add_convert_fusion.3.refs_1_
  535.6 0.6 maximum_bitcast_fusion.1.refs_0_
  536.2 27.3 %gather_sums.1 = (f32[16,2,32,128]{3,2,1,0:T(8,128)}, bf16[128,1536]{1,0:T(8,128)(2,1)}) custom-call(f32[1,32,128]{2,1,0:T(8,128)} %maximum_bitcast_fusion.1.refs_0_, bf16[128,1536]{1,0:T(8,128)(2,1)} %add_convert_fusion.3.refs_1_), custom_call_target="tpu_custom_call" | custom-call | tf_op jit(solution)/shard_map/gather_sums/pallas_call | solution.py:125
  563.5 1.5 reshape.290
  565.2 0.2 slice_reduce_fusion.1
  565.4 0.6 fusion.36
  566.0 2.5 maximum_select_fusion.1
  568.5 0.6 slice.138
  569.1 0.5 fusion.35
  569.6 2.2 maximum_select_fusion
  571.8 0.8 slice_bitcast_fusion.3
  572.7 0.6 fusion.33
  573.3 0.3 convert_element_type.114
  573.7 2.4 slice_bitcast_fusion
  (87 shorter events, 1.5 us)
Async XLA Ops:
  0.6 44.0 %copy-start.24 = (bf16[1536]{0:T(1024)(128)(2,1)S(1)}, bf16[1536]{0:T(1024)(128)(2,1)}, u32[]{:S(2)}) copy-start(bf16[1536]{0:T(1024)(128)(2,1)} %param.18) | copy-start | bytes 9220
  0.7 44.0 %copy-start.3 = (bf16[256,1536]{1,0:T(8,128)(2,1)S(1)}, bf16[256,1536]{1,0:T(8,128)(2,1)}, u32[]{:S(2)}) copy-start(bf16[256,1536]{1,0:T(8,128)(2,1)} %param.17) | copy-start | bytes 2359300
  2.5 42.4 %copy-start.27 = (bf16[768]{0:T(1024)(128)(2,1)S(1)}, bf16[768]{0:T(1024)(128)(2,1)}, u32[]{:S(2)}) copy-start(bf16[768]{0:T(1024)(128)(2,1)} %param.20) | copy-start | bytes 4612
  2.5 42.4 %copy-start.29 = (bf16[128]{0:T(256)(128)(2,1)S(1)}, bf16[128]{0:T(256)(128)(2,1)}, u32[]{:S(2)}) copy-start(bf16[128]{0:T(256)(128)(2,1)} %param.24) | copy-start | bytes 772
  2.5 42.4 %copy-start.30 = (bf16[128]{0:T(256)(128)(2,1)S(1)}, bf16[128]{0:T(256)(128)(2,1)}, u32[]{:S(2)}) copy-start(bf16[128]{0:T(256)(128)(2,1)} %param.22) | copy-start | bytes 772
  44.9 3.0 copy-start.25
  47.9 1.0 copy-start.6
  48.9 0.7 copy-start.31
  51.0 0.7 copy-start.15
  52.0 4.3 copy-start.28
  54.6 59.1 %copy-start.16 = (bf16[4480,96]{0,1:T(8,128)(2,1)S(1)}, bf16[4480,96]{0,1:T(8,128)(2,1)}, u32[]{:S(2)}) copy-start(bf16[4480,96]{0,1:T(8,128)(2,1)} %param.29) | copy-start | bytes 2580484
  112.2 4.9 copy-start.23
  231.0 9.4 %copy-start.1 = (bf16[16,1,128,1536]{3,2,1,0:T(8,128)(2,1)S(1)}, bf16[16,1,128,1536]{3,2,1,0:T(8,128)(2,1)}, u32[]{:S(2)}) copy-start(bf16[16,1,128,1536]{3,2,1,0:T(8,128)(2,1)} %get-tuple-element.38) | copy-start | bytes 18874372
  231.0 9.4 %copy-start.2 = (bf16[3,1536,640]{2,1,0:T(8,128)(2,1)S(1)}, bf16[3,1536,640]{2,1,0:T(8,128)(2,1)}, u32[]{:S(2)}) copy-start(bf16[3,1536,640]{2,1,0:T(8,128)(2,1)} %get-tuple-element.37.refs_6_) | copy-start | bytes 17694724
  257.4 8.2 %copy-start.9 = (bf16[2048,640]{1,0:T(8,128)(2,1)}, bf16[2048,640]{1,0:T(8,128)(2,1)S(1)}, u32[]{:S(2)}) copy-start(bf16[2048,640]{1,0:T(8,128)(2,1)S(1)} %get-tuple-element.63.refs_3_) | copy-start | bytes 7864324
  257.4 8.2 %copy-start.10 = (bf16[2048,640]{1,0:T(8,128)(2,1)}, bf16[2048,640]{1,0:T(8,128)(2,1)S(1)}, u32[]{:S(2)}) copy-start(bf16[2048,640]{1,0:T(8,128)(2,1)S(1)} %get-tuple-element.64.refs_4_) | copy-start | bytes 7864324
  275.7 59.6 %copy-start = (f32[128,1536]{1,0:T(8,128)S(1)}, f32[128,1536]{1,0:T(8,128)}, u32[]{:S(2)}) copy-start(f32[128,1536]{1,0:T(8,128)} %get-tuple-element.35) | copy-start | bytes 2359300
  275.7 61.2 %copy-start.17 = (bf16[256,1536]{1,0:T(8,128)(2,1)S(1)}, bf16[256,1536]{1,0:T(8,128)(2,1)}, u32[]{:S(2)}) copy-start(bf16[256,1536]{1,0:T(8,128)(2,1)} %param.33) | copy-start | bytes 2359300
  457.9 3.2 copy-start.21
  461.1 0.8 copy-start.5
  461.8 0.6 copy-start.20
  465.4 0.8 copy-start.12
  466.2 3.8 copy-start.22
  466.2 3.8 copy-start.26
  470.0 2.3 copy-start.8
  470.0 2.3 copy-start.18
  532.8 1.7 copy-start.7
  532.8 1.7 copy-start.14
  533.0 2.5 copy-start.13
  534.4 35.2 %copy-start.4 = (bf16[128,1536]{1,0:T(8,128)(2,1)S(1)}, bf16[128,1536]{1,0:T(8,128)(2,1)}, u32[]{:S(2)}) copy-start(bf16[128,1536]{1,0:T(8,128)(2,1)} %add_convert_fusion.4.refs_2_) | copy-start | bytes 1179652
  563.5 9.8 %copy-start.11 = (bf16[3,96,4480]{2,1,0:T(8,128)(2,1)S(1)}, bf16[3,96,4480]{2,1,0:T(8,128)(2,1)}, u32[]{:S(2)}) copy-start(bf16[3,96,4480]{2,1,0:T(8,128)(2,1)} %get-tuple-element.53) | copy-start | bytes 7741444
  566.0 5.8 %copy-start.19 = (f32[96,1792]{1,0:T(8,128)S(1)}, f32[96,1792]{1,0:T(8,128)}, u32[]{:S(2)}) copy-start(f32[96,1792]{1,0:T(8,128)} %get-tuple-element.52) | copy-start | bytes 2064388

commit v4 on v3

--- a/solution.py
+++ b/solution.py
@@ -134,7 +134,7 @@
     return split(flat, n_out)
 
 
-def gather(x, count, tower=False, pieces=1, both=False):
+def gather(x, count, tower=False, pieces=1, both=False, flat=False):
     lines, columns = grid_of(count)
     across = 2 if tower else columns
     members = lines * across * 2
@@ -166,8 +166,13 @@
         core, col, row = grid.core, grid.col, grid.row
         me = grid.index(row, col, core)
 
+        def spot(shard, piece):
+            if flat:
+                return o_ref.at[pl.ds(pl.multiple_of(shard * shape[0], shape[0]), shape[0])]
+            return o_ref.at[shard, piece]
+
         def copy(hop, shard, piece, src):
-            return remote(src, o_ref.at[shard, piece], send.at[hop, shard, piece], recv.at[shard, piece], hops[hop][1])
+            return remote(src, spot(shard, piece), send.at[hop, shard, piece], recv.at[shard, piece], hops[hop][1])
 
         order = sorted(
             ((dr, dq) for dr in range(1 - lines, lines) for dq in range(1 - across, across)),
@@ -179,7 +184,9 @@
             )
             pair.start()
         sends = []
-        mine = pltpu.make_async_copy(x_ref, o_ref.at[me, pl.ds(0, pieces)], local)
+        mine = pltpu.make_async_copy(
+            x_ref.at[0] if flat else x_ref, spot(me, 0) if flat else o_ref.at[me, pl.ds(0, pieces)], local
+        )
         for dr, dq in order:
             shard = grid.index(row - dr, col - dq, core)
             valid = (row - dr >= 0) & (row - dr < lines) & (col - dq >= 0) & (col - dq < across)
@@ -196,7 +203,7 @@
             onward.append(4)
             for piece in range(copies):
                 own = dr == 0 and dq == 0
-                src = o_ref.at[shard, piece]
+                src = spot(shard, piece)
                 if own and piece < pieces:
                     src = x_ref.at[piece]
                 if own and piece >= pieces:
@@ -223,7 +230,7 @@
             for q in range(across):
                 for piece in range(copies):
                     shard = grid.index(r, q, 1 - core)
-                    copy(4, shard, piece, o_ref.at[shard, piece]).wait_recv()
+                    copy(4, shard, piece, spot(shard, piece)).wait_recv()
         yield True
         for go, hop, shard, piece, src in sends:
 
@@ -238,8 +245,8 @@
     return Task(
         [x],
         [VMEM],
-        [jax.ShapeDtypeStruct((members, copies) + x.shape[1:], x.dtype)],
-        [HBM],
+        [jax.ShapeDtypeStruct((members * shape[0],) + shape[1:] if flat else (members, copies) + x.shape[1:], x.dtype)],
+        [VMEM if flat else HBM],
         [dma((5, members, copies)), dma((members, copies)), dma, dma((2,))],
         targets,
         run,
@@ -506,12 +513,13 @@
                 grid.where(grid.row, (grid.column + e) % columns, grid.core),
             )
 
-        for slot in range(slots):
+        def begin(slot):
             for e in range(1, members):
                 guarded(full(slot, mine ^ e), lambda: out(slot, e).start())
             guarded(
                 full(slot, mine), lambda: pltpu.make_async_copy(block(slot, mine), spot(slot), recv.at[slot]).start()
             )
+
         last = slots - 1
         some = full(last, mine)
         if some is not True:
@@ -528,9 +536,7 @@
                 for fill in fills:
                     fill.wait()
 
-        yield True
-        for slot in range(slots):
-
+        def relay(slot):
             def pass_on():
                 pltpu.make_async_copy(bytes_of(slot), bytes_of(slot), recv.at[slot]).wait()
                 for r in range(lines):
@@ -538,7 +544,17 @@
                         over(slot, r, e).start()
 
             guarded(full(slot, mine), pass_on)
+
+        lead = min(3, slots)
+        for slot in range(lead):
+            begin(slot)
             yield True
+        for slot in range(slots):
+            relay(slot)
+            yield True
+            if slot + lead < slots:
+                begin(slot + lead)
+                yield True
         for slot in range(slots):
 
             def finish():
@@ -749,19 +765,55 @@
     )
 
 
-def forward(most, count, begin, q, kv, attn, x, gain):
-    tokens, width = q.shape[0], x.shape[1]
-    part, inner = x.shape[0], q.shape[1]
+def forward(most, count, begin, weights, rows_in, bias, cosine, sine, x, gain):
+    tokens, width = rows_in.shape
+    part, pre_cols = x.shape[0], bias.shape[1]
+    inner = pre_cols - 2 * HEAD_SIZE
+    matrix = gather(weights, count, flat=True)
+    keys = gather(jax.ShapeDtypeStruct((tokens, 2 * HEAD_SIZE), jnp.bfloat16), count, flat=True)
+    q = jax.ShapeDtypeStruct((tokens, inner), jnp.bfloat16)
+    kv = keys.outs[0]
     core = attend(most, begin, q, kv)
     rows = gather(jax.ShapeDtypeStruct((part, width), jnp.bfloat16), count, tower=True)
     pair = swap([jax.ShapeDtypeStruct((part, width), jnp.bfloat16)])
-    n_rows, n_pair = len(rows.scratch), len(pair.scratch)
+    n_pair, n_matrix, n_keys = len(pair.scratch), len(matrix.scratch), len(keys.scratch)
     columns = 256
-    skip = attn.shape[1] - inner
-
-    def run(begin_ref, q_ref, kv_ref, attn_ref, x_ref, gain_ref, o_ref, lse_ref, hidden_ref, rows_ref, *scratch):
-        sent, got, normed, whole = scratch[:4]
+    skip = weights.shape[1] - inner
+
+    def run(
+        begin_ref, w_ref, in_ref, bias_ref, cos_ref, sin_ref, x_ref, gain_ref,
+        attn_ref, q_ref, kv_ref, o_ref, lse_ref, hidden_ref, rows_ref, *scratch
+    ):
+        sent, got, normed, whole, own = scratch[:5]
+        scratch = scratch[5:]
         half = lax.axis_index("head")
+        yield from matrix.run(w_ref, attn_ref, *scratch[:n_matrix])
+        scratch = scratch[n_matrix:]
+
+        def turned(value):
+            return value * cos_ref[...] + pltpu.roll(value, HEAD_SIZE // 2, 1) * sin_ref[...]
+
+        def pre_of(start):
+            cols = pl.ds(start, 2 * HEAD_SIZE)
+            return (
+                jnp.dot(in_ref[...], attn_ref[:, cols], preferred_element_type=jnp.float32) + bias_ref[:, cols]
+            )
+
+        def two_heads(i, carry):
+            start = pl.multiple_of(i * 2 * HEAD_SIZE, 2 * HEAD_SIZE)
+            pre = pre_of(start)
+            q_ref[:, pl.ds(start, HEAD_SIZE)] = turned(pre[:, :HEAD_SIZE]).astype(q_ref.dtype)
+            q_ref[:, pl.ds(start + HEAD_SIZE, HEAD_SIZE)] = turned(pre[:, HEAD_SIZE:]).astype(q_ref.dtype)
+            return carry
+
+        pre = pre_of(inner)
+        own[0, :, :HEAD_SIZE] = turned(pre[:, :HEAD_SIZE]).astype(own.dtype)
+        own[0, :, HEAD_SIZE:] = pre[:, HEAD_SIZE:].astype(own.dtype)
+        for step, _ in enumerate(keys.run(own, kv_ref, *scratch[:n_keys])):
+            if step == 0:
+                lax.fori_loop(0, inner // (2 * HEAD_SIZE), two_heads, 0)
+            yield True
+        scratch = scratch[n_keys:]
         yield from core.run(begin_ref, q_ref, kv_ref, o_ref, lse_ref)
 
         def project(i, carry):
@@ -780,7 +832,7 @@
             return pl.ds(pl.multiple_of(h * part, part), part)
 
         sent[...] = whole[of(1 - half)].astype(jnp.bfloat16)
-        yield from pair.run(sent, got, *scratch[4 : 4 + n_pair])
+        yield from pair.run(sent, got, *scratch[:n_pair])
         step = 16
 
         def norm(i, carry):
@@ -792,22 +844,25 @@
             return carry
 
         lax.fori_loop(0, part // step, norm, 0)
-        yield from rows.run(normed, rows_ref, *scratch[4 + n_pair :])
+        yield from rows.run(normed, rows_ref, *scratch[n_pair:])
 
     def targets():
-        return pair.targets() + rows.targets()
+        return matrix.targets() + pair.targets() + rows.targets()
 
     return Task(
-        [begin, q, kv, attn, x, gain],
-        [VMEM] * 6,
-        core.outs + [jax.ShapeDtypeStruct((part, width), jnp.float32)] + rows.outs,
-        [VMEM] * 3 + rows.out_specs,
+        [begin] + matrix.inputs + [rows_in, bias, cosine, sine, x, gain],
+        [VMEM] * 8,
+        matrix.outs + [q, kv] + core.outs + [jax.ShapeDtypeStruct((part, width), jnp.float32)] + rows.outs,
+        [VMEM] * 6 + rows.out_specs,
         [
             pltpu.VMEM((part, width), jnp.bfloat16),
             pltpu.VMEM((part, width), jnp.bfloat16),
             pltpu.VMEM((1, part, width), jnp.bfloat16),
             pltpu.VMEM((tokens, width), jnp.float32),
+            pltpu.VMEM((1, tokens, 2 * HEAD_SIZE), jnp.bfloat16),
         ]
+        + matrix.scratch
+        + keys.scratch
         + pair.scratch
         + rows.scratch,
         targets,
@@ -1106,39 +1161,44 @@
         jnp.sum(jnp.where(picked, source_weights[None, :], 0), axis=1).astype(f32) / loss_denominator
     )
     cotangent = mine(out_grad).astype(f32) * mine(row_scale[:, None])
-    ((attn_full,),) = fuse(1, "gather_weights", gather(attn_local, count))
-    attn_full = attn_full.reshape(width, -1)
     qkv_cols = q_cols + 2 * kv_cols
-    full_qkv = attn_full[:, :qkv_cols]
-    full_o = attn_full[:, qkv_cols:]
     inputs = layer_in.astype(f32)
     scale_one = rms_scale(inputs)
     gain_one = gain_attn.astype(f32)
     normed = (inputs * scale_one * gain_one).astype(bf16)
     bias = jnp.concatenate([q_bias, key_bias, value_bias]).astype(f32)
-    pre = dot(normed, full_qkv) + bias
-    turned = rotary_apply(
-        pre[:, : q_cols + kv_cols].reshape(tok_rows, heads + 1, HEAD_SIZE), cosine_table, sine_table
-    ).reshape(tok_rows, q_cols + kv_cols)
-    query_rows = turned[:, :q_cols].astype(bf16)
-    kv_rows = jnp.concatenate([turned[:, q_cols:], pre[:, q_cols + kv_cols :]], axis=1).astype(bf16)
-    ((kv_all,), (grad_all,)) = fuse(
-        2, "gather_keys", gather(kv_rows, count), gather(cotangent.astype(bf16), count, tower=True)
-    )
-    grad_all = grad_all.reshape(-1, width)
-    kv_all = kv_all.reshape(-1, 2 * kv_cols)
     begin = doc_begin[:, None].astype(jnp.int32)
     most = longest(count * tok_rows)
     mlp_local = jnp.stack([gate_weight, up_weight, down_weight.T])
     gain_two = gain_mlp.astype(f32)
-    ahead = (0, 1) + (1, 1, 1, 0) + (1, 1, 1, 0) + (1, 0, 1, 1, 0) + (1,) * 6 + (0,)
-    ((mlp_full,), (attended_raw, row_lse, hidden, rows_all)) = fuse(
+    signed_sine = jnp.concatenate([-sine_table[:, 0, : HEAD_SIZE // 2], sine_table[:, 0, HEAD_SIZE // 2 :]], axis=1)
+    ahead = (
+        (1,) * 8 + (0,) + (1,) * 7 + (0,) + (1,) * 7 + (0, 2, 0)
+        + (1,) * 8 + (0,) + (1,) * 14 + (2, 2, 2, 1)
+        + (1, 0, 1, 2, 2, 0, 1, 0, 2, 2, 1, 2, 2, 2, 0, 1, 2, 2, 2, 1, 2, 2, 0)
+        + (1, 2, 2, 2, 1) + (1, 2) * 24
+    )
+    ((mlp_full,), (attn_full, query_rows, kv_all, attended_raw, row_lse, hidden, rows_all), (grad_all,)) = fuse(
         3,
-        "forward_spread",
+        "forward",
         spread(mlp_local, count),
-        forward(most, count, begin, query_rows, kv_all, attn_full, mine(layer_in), gain_two[None, :]),
+        forward(
+            most,
+            count,
+            begin,
+            attn_local,
+            normed,
+            bias[None, :],
+            cosine_table[:, 0, :],
+            signed_sine,
+            mine(layer_in),
+            gain_two[None, :],
+        ),
+        gather(cotangent.astype(bf16), count, tower=True),
         order=ahead,
     )
+    grad_all = grad_all.reshape(-1, width)
+    full_qkv = attn_full[:, :qkv_cols]
     attended = attended_raw.astype(bf16)
     scale_two = rms_scale(hidden)
     rows_all = rows_all.reshape(-1, width)

time: 584 us -> 562 us (0.962)
  Pallas kernels: 470 us -> 454 us
    pallas_call x7 -> x5, Pallas kernels: 470 us -> 454 us  [fuse(): pl.pallas_call(kernel, out_shape=[o for t in tasks for o in t.outs], in_s...]
    dot_general x9 -> x8, matrix products: 53.6 us -> 50.7 us  [dot(): lax.dot_general(a, b, (dims, ((), ())), preferred_element_type=jnp.float32)]
where the time goes in v4:
time: 562 us; the launch traced here: 555 us
  Pallas kernels  454 us (81%)
  matrix products  50.7 us (9%)
  other arithmetic  32.1 us (6%)
  local copies, waits for them, and re-layouts  17 us (3%)
    pallas_call x5, Pallas kernels, fuse(): pl.pallas_call(kernel, out_shape=[o for t in tasks for o in t.outs], in_s...  454 us
    dot_general x8, matrix products, dot(): lax.dot_general(a, b, (dims, ((), ())), preferred_element_type=jnp.float32)  50.7 us

profile of v4, /device:TPU:1, one launch (start us, length us, event | category | flops | bytes accessed | tf_op | source)
XLA Modules:
  0.0 554.8 jit_solution(1092869855630034369)
XLA Ops:
  0.7 0.9 select_reduce_fusion
  1.7 1.9 fusion.18.refs_9_
  3.6 0.8 reduce-window.9
  4.4 0.7 bitcast_subtract_fusion
  5.2 0.1 fusion.23
  5.3 0.5 maximum_sine_fusion
  5.8 0.1 fusion.20
  5.9 1.3 fusion.21
  7.2 1.8 constant_dynamic-slice_fusion.refs_7_
  9.0 0.2 multiply_reduce_fusion
  9.3 0.6 copy-done.27
  9.8 1.1 multiply_convert_fusion.3.refs_3_
  10.9 0.8 copy.38.refs_1_
  11.8 1.9 pad_maximum_fusion.1.refs_0_
  13.7 0.8 maximum_bitcast_fusion.refs_2_
  14.4 0.7 concatenate.80
  15.1 1.3 maximum_convert_fusion.1.refs_4_
  16.4 0.6 broadcast_in_dim.28.refs_8_
  17.0 190.0 %forward.1 = (bf16[3,1536,640]{2,1,0:T(8,128)(2,1)}, bf16[1536,1792]{1,0:T(8,128)(2,1)}, bf16[256,768]{1,0:T(8,128)(2,1)}, bf16[4096,256]{1,0:T(8,128)(2,1)}, f3...) custom-call(bf16[3,96,4480]{2,1,0:T(8,128)(2,1)} %pad_maximum_fusion, ...), custom_call_target="tpu_custom_call" | custom-call | tf_op jit(solution)/shard_map/forward/pallas_call | solution.py:125
  207.0 9.4 %fusion.10 = f32[2048,640]{1,0:T(8,128)} fusion(bf16[2048,1536]{1,0:T(8,128)(2,1)} %bitcast.77, bf16[3,1536,640]{2,1,0:T(8,128)(2,1)} %get-tuple-element.38.refs_6_), kind=kOutput, calls=%fused_computation.19 | convolution fusion | flops 4026531840 | bytes 13500416 | tf_op jit(solution)/shard_map/dot_general | solution.py:991
  216.4 6.8 %fusion.5 = f32[2048,640]{1,0:T(8,128)} fusion(bf16[2048,1536]{1,0:T(8,128)(2,1)S(1)} %bitcast.75, bf16[3,1536,640]{2,1,0:T(8,128)(2,1)S(1)} %copy-done.4), kind=kOutput, calls=%fused_computation.14 | convolution fusion | flops 4026531840 | bytes 13500416 | tf_op jit(solution)/shard_map/dot_general | solution.py:991
  223.2 10.2 %multiply_convert_fusion = (bf16[2048,640]{1,0:T(8,128)(2,1)}, bf16[2048,640]{1,0:T(8,128)(2,1)S(1)}, bf16[2048,640]{1,0:T(8,128)(2,1)S(1)}) fusion(f32[2048,640]{1,0:T(8,128)} %fusion.5, f32[2048,640]{1,0:T(8,128)} %fusion.10, bf16[2048,1536]{1,0:T(8,128)(2,1)S(1)} %bitcast.76, bf16[3,1536,640]{2,1,0:T(8,128)(2,1)S(1)} %copy-done.4), kind=kOutput, calls=%fused_computation.2 | convolution fusion | flops 4046192640 | bytes 26607616 | tf_op jit(solution)/shard_map/dot_general | solution.py:991
  233.3 8.1 %fusion.3 = f32[2048,1536]{1,0:T(8,128)} fusion(bf16[2048,640]{1,0:T(8,128)(2,1)S(1)} %get-tuple-element.67.refs_3_, bf16[3,1536,640]{2,1,0:T(8,128)(2,1)S(1)} %copy-done.4), kind=kOutput, calls=%fused_computation.12 | convolution fusion | flops 4026531840 | bytes 17170432 | tf_op jit(solution)/shard_map/dot_general | solution.py:991
  241.5 10.3 %add_convert_fusion = bf16[2048,1536]{1,0:T(8,128)(2,1)} fusion(f32[2048,1536]{1,0:T(8,128)} %fusion.3, bf16[2048,640]{1,0:T(8,128)(2,1)S(1)} %get-tuple-element.68.refs_4_, bf16[3,1536,640]{2,1,0:T(8,128)(2,1)S(1)} %copy-done.4), kind=kOutput, calls=%fused_computation | convolution fusion | flops 4032823296 | bytes 23461888 | tf_op jit(solution)/shard_map/dot_general | solution.py:991
  251.8 58.4 %scatter_grads.1 = (f32[128,1536]{1,0:T(8,128)}, bf16[3,1536,640]{2,1,0:T(8,128)(2,1)}, bf16[2048,1536]{1,0:T(8,128)(2,1)}) custom-call(bf16[16,128,1536]{2,1,0:T(8,128)(2,1)} %bitcast.79, bf16[2048,1536]{1,0:T(8,128)(2,1)} %bitcast.74, bf16[2048,1536]{1,0:T(8,128)(2,1)} %bitcast.78, bf16[2048,640]{1,0:T(8,128)(2,1)} %copy-done.8, ...), custom_call_target="tpu_custom_call" | custom-call | tf_op jit(solution)/shard_map/scatter_grads/pallas_call | solution.py:125
  310.2 0.1 multiply_reduce_fusion.5
  310.4 1.4 multiply_reduce_fusion.1
  311.8 2.5 fusion.27
  314.2 123.4 %backward_collect.1 = (bf16[3,96,4480]{2,1,0:T(8,128)(2,1)}, f32[256,768]{1,0:T(8,128)}, f32[256,256]{1,0:T(8,128)}, bf16[256,1536]{1,0:T(8,128)(2,1)}, f32[128,1536]{1,0:T(8,128)}) custom-call(bf16[3,1536,640]{2,1,0:T(8,128)(2,1)} %get-tuple-element.40.refs_0_, s32[256,1]{1,0:T(8,128)} %copy.38.refs_1_, bf16[256,768]{1,0:T(8,128)(2,1)} %get-tuple-element.41.refs_2_, ...), custom_call_target="tpu_custom_call" | custom-call | tf_op jit(solution)/shard_map/backward_collect/pallas_call | solution.py:125
  437.7 2.0 add_convert_fusion.3.refs_2_
  439.7 1.2 multiply_convert_fusion.4
  441.0 0.3 copy.42
  441.3 0.1 copy.43
  441.5 0.1 fusion.28
  441.7 0.3 copy.44
  442.0 1.0 copy.40
  443.1 1.2 copy.41
  444.3 1.3 add_convert_fusion.1
  445.6 4.1 fusion.1
  449.8 1.9 dynamic-slice_convert_fusion.refs_1_
  451.7 1.0 convolution_convert_fusion
  452.7 0.1 copy-done.7
  452.8 0.2 copy-done.17
  453.1 0.8 convolution_convert_fusion.1
  453.9 2.9 pad_maximum_fusion.refs_0_
  456.8 57.2 %scatter_last.1 = (f32[96,1792]{1,0:T(8,128)}, bf16[128,1536]{1,0:T(8,128)(2,1)}, bf16[128,1536]{1,0:T(8,128)(2,1)}) custom-call(bf16[16,96,1792]{2,1,0:T(8,128)(2,1)} %pad_maximum_fusion.refs_0_, bf16[128,1536]{1,0:T(8,128)(2,1)} %dynamic-slice_convert_fusion.refs_1_, bf16[128,1536]{1,0:T(8,128)(2,1)} %add_convert_fusion.3.refs_2_), custom_call_target="tpu_custom_call" | custom-call | tf_op jit(solution)/shard_map/scatter_last/pallas_call | solution.py:125
  514.1 0.2 convert_element_type.86
  514.3 1.3 multiply_reduce_fusion.3
  515.7 1.0 add_convert_fusion.2.refs_1_
  516.7 0.1 convert_reduce_fusion
  516.8 0.6 maximum_bitcast_fusion.1.refs_0_
  517.4 24.6 %gather_sums.1 = (f32[16,2,32,128]{3,2,1,0:T(8,128)}, bf16[128,1536]{1,0:T(8,128)(2,1)}) custom-call(f32[1,32,128]{2,1,0:T(8,128)} %maximum_bitcast_fusion.1.refs_0_, bf16[128,1536]{1,0:T(8,128)(2,1)} %add_convert_fusion.2.refs_1_), custom_call_target="tpu_custom_call" | custom-call | tf_op jit(solution)/shard_map/gather_sums/pallas_call | solution.py:125
  542.0 1.5 reshape.304
  543.5 0.1 slice_reduce_fusion
  543.6 0.2 slice_reduce_fusion.1
  543.9 0.6 fusion.32
  544.5 2.5 maximum_select_fusion.1
  547.0 0.6 slice.114
  547.6 0.5 fusion.31
  548.1 2.2 maximum_select_fusion
  550.3 0.8 slice_bitcast_fusion.3
  551.2 0.6 fusion.29
  551.8 0.3 convert_element_type.108
  552.2 2.4 slice_bitcast_fusion
  (81 shorter events, 0.8 us)
Async XLA Ops:
  0.6 8.3 %copy-start.2 = (bf16[256,1536]{1,0:T(8,128)(2,1)S(1)}, bf16[256,1536]{1,0:T(8,128)(2,1)}, u32[]{:S(2)}) copy-start(bf16[256,1536]{1,0:T(8,128)(2,1)} %param.17) | copy-start | bytes 2359300
  0.7 8.3 %copy-start.29 = (bf16[1536]{0:T(1024)(128)(2,1)S(1)}, bf16[1536]{0:T(1024)(128)(2,1)}, u32[]{:S(2)}) copy-start(bf16[1536]{0:T(1024)(128)(2,1)} %param.18) | copy-start | bytes 9220
  0.7 11.1 %copy-start.15 = (bf16[96,4480]{1,0:T(8,128)(2,1)S(1)}, bf16[96,4480]{1,0:T(8,128)(2,1)}, u32[]{:S(2)}) copy-start(bf16[96,4480]{1,0:T(8,128)(2,1)} %param.27) | copy-start | bytes 2580484
  0.7 11.1 %copy-start.14 = (bf16[96,4480]{1,0:T(8,128)(2,1)S(1)}, bf16[96,4480]{1,0:T(8,128)(2,1)}, u32[]{:S(2)}) copy-start(bf16[96,4480]{1,0:T(8,128)(2,1)} %param.28) | copy-start | bytes 2580484
  0.7 11.1 %copy-start.13 = (bf16[4480,96]{0,1:T(8,128)(2,1)S(1)}, bf16[4480,96]{0,1:T(8,128)(2,1)}, u32[]{:S(2)}) copy-start(bf16[4480,96]{0,1:T(8,128)(2,1)} %param.29) | copy-start | bytes 2580484
  1.7 7.3 %copy-start.30 = (f32[128]{0:T(128)}, f32[128]{0:T(128)S(1)}, u32[]{:S(2)}) copy-start(f32[128]{0:T(128)S(1)} %dynamic-slice.6) | copy-start | bytes 1540
  9.2 0.6 copy-start.27
  9.8 3.8 copy-start.22
  9.8 3.8 copy-start.24
  10.9 5.4 copy-start.26
  11.7 1.9 copy-start.23
  11.7 1.9 copy-start.25
  206.9 9.4 %copy-start.3 = (bf16[16,1,128,1536]{3,2,1,0:T(8,128)(2,1)S(1)}, bf16[16,1,128,1536]{3,2,1,0:T(8,128)(2,1)}, u32[]{:S(2)}) copy-start(bf16[16,1,128,1536]{3,2,1,0:T(8,128)(2,1)} %get-tuple-element.39) | copy-start | bytes 18874372
  207.0 9.4 %copy-start.4 = (bf16[3,1536,640]{2,1,0:T(8,128)(2,1)S(1)}, bf16[3,1536,640]{2,1,0:T(8,128)(2,1)}, u32[]{:S(2)}) copy-start(bf16[3,1536,640]{2,1,0:T(8,128)(2,1)} %get-tuple-element.38.refs_6_) | copy-start | bytes 17694724
  233.3 8.1 %copy-start.8 = (bf16[2048,640]{1,0:T(8,128)(2,1)}, bf16[2048,640]{1,0:T(8,128)(2,1)S(1)}, u32[]{:S(2)}) copy-start(bf16[2048,640]{1,0:T(8,128)(2,1)S(1)} %get-tuple-element.67.refs_3_) | copy-start | bytes 7864324
  233.3 8.1 %copy-start.9 = (bf16[2048,640]{1,0:T(8,128)(2,1)}, bf16[2048,640]{1,0:T(8,128)(2,1)S(1)}, u32[]{:S(2)}) copy-start(bf16[2048,640]{1,0:T(8,128)(2,1)S(1)} %get-tuple-element.68.refs_4_) | copy-start | bytes 7864324
  251.8 58.5 %copy-start = (f32[128,1536]{1,0:T(8,128)S(1)}, f32[128,1536]{1,0:T(8,128)}, u32[]{:S(2)}) copy-start(f32[128,1536]{1,0:T(8,128)} %get-tuple-element.36) | copy-start | bytes 2359300
  251.8 60.0 %copy-start.16 = (bf16[256,1536]{1,0:T(8,128)(2,1)S(1)}, bf16[256,1536]{1,0:T(8,128)(2,1)}, u32[]{:S(2)}) copy-start(bf16[256,1536]{1,0:T(8,128)(2,1)} %param.33) | copy-start | bytes 2359300
  251.8 60.0 %copy-start.31 = (f32[128]{0:T(128)S(1)}, f32[128]{0:T(128)}, u32[]{:S(2)}) copy-start(f32[128]{0:T(128)} %copy-done.30) | copy-start | bytes 1540
  437.6 3.2 copy-start.21
  437.7 3.7 copy-start.20
  440.9 0.7 copy-start.19
  445.6 6.1 %copy-start.1 = (bf16[256,1536]{1,0:T(8,128)(2,1)S(1)}, bf16[256,1536]{1,0:T(8,128)(2,1)}, u32[]{:S(2)}) copy-start(bf16[256,1536]{1,0:T(8,128)(2,1)} %multiply_convert_fusion.3.refs_3_) | copy-start | bytes 2359300
  451.7 1.1 copy-start.7
  451.7 1.4 copy-start.17
  456.8 57.2 %copy-start.28 = (f32[256]{0:T(256)S(1)}, f32[256]{0:T(256)}, u32[]{:S(2)}) copy-start(f32[256]{0:T(256)} %copy-done.27) | copy-start | bytes 3076
  456.8 57.5 %copy-start.11 = (f32[256,1536]{1,0:T(8,128)S(1)}, f32[256,1536]{1,0:T(8,128)}, u32[]{:S(2)}) copy-start(f32[256,1536]{1,0:T(8,128)} %fusion.1) | copy-start | bytes 4718596
  514.0 1.6 copy-start.6
  514.0 1.6 copy-start.12
  515.7 32.4 %copy-start.5 = (bf16[128,1536]{1,0:T(8,128)(2,1)S(1)}, bf16[128,1536]{1,0:T(8,128)(2,1)}, u32[]{:S(2)}) copy-start(bf16[128,1536]{1,0:T(8,128)(2,1)} %add_convert_fusion.3.refs_2_) | copy-start | bytes 1179652
  542.0 9.8 %copy-start.10 = (bf16[3,96,4480]{2,1,0:T(8,128)(2,1)S(1)}, bf16[3,96,4480]{2,1,0:T(8,128)(2,1)}, u32[]{:S(2)}) copy-start(bf16[3,96,4480]{2,1,0:T(8,128)(2,1)} %get-tuple-element.57) | copy-start | bytes 7741444
  544.5 5.8 %copy-start.18 = (f32[96,1792]{1,0:T(8,128)S(1)}, f32[96,1792]{1,0:T(8,128)}, u32[]{:S(2)}) copy-start(f32[96,1792]{1,0:T(8,128)} %get-tuple-element.56) | copy-start | bytes 2064388
